TPU v7x, 256 devices: a 8x8x2 block of a 8x8x16 slice. The times are simulated.
256 devices in a mesh: parts: 2 (over z), seq: 128 (over x, y, core).
Axes of the slice: x: 8, y: 8, z: 2, core: 2. Of those that a mesh axis runs over, the one named last changes fastest.
The devices are a block of a 8x8x16 slice.
Arguments:
- token_ids: int32 [4, 4], P(None, 'parts'), parts along dimension 1, may hold values from 0 to 76031
- lengths: int32 [4], P('parts'), parts along dimension 0, may hold values from 24576 to 32768, as said below
- embed_table: bfloat16 [76032, 5120], P('seq'), may hold values from -6 to 6
- attn_gain: bfloat16 [5120], replicated, may hold values from 0.25 to 1.75
- w_qkv: bfloat16 [5120, 7168], P('seq'), may hold values from -0.3125 to 0.3125
- qkv_bias: float32 [7168], replicated, may hold values from -8 to 8
- cache_keys: bfloat16 [4, 32768, 1024], P('parts', 'seq'), parts along dimension 0, may hold values from -300 to 300
- cache_values: bfloat16 [4, 32768, 1024], P('parts', 'seq'), parts along dimension 0, may hold values from -6 to 6
- w_out: bfloat16 [5120, 5120], P(None, 'seq'), may hold values from -0.078125 to 0.078125
- mlp_gain: bfloat16 [5120], replicated, may hold values from 0.25 to 1.75
- w_gate: bfloat16 [5120, 16384], P(None, 'seq'), may hold values from -0.078125 to 0.078125
- w_up: bfloat16 [5120, 16384], P(None, 'seq'), may hold values from -0.078125 to 0.078125
- w_down: bfloat16 [16384, 5120], P('seq'), may hold values from -0.1875 to 0.1875
Outputs:
- attended: bfloat16 [4, 4, 5120], P(None, 'parts'), parts along dimension 1
- layer_out: bfloat16 [4, 4, 5120], P(None, 'parts', 'seq'), parts along dimension 1
There are 2 independent parts, one for each index of `parts`. A program takes and returns all parts, laid end to end along the dimension named above; an argument that names none is the same for every part. Nothing has to cross between parts.
Inputs may be any that keep to these rules, and one draw needn't show every extreme that they name: Cache positions lengths[b] and later are unused; the first prompt fills the whole cache of 32768 positions.
All inputs are finite; a program needn't handle non-finite values.
Results may differ from a plain program's by a relative error of at most 0.017.
The roundings to bfloat16 on the way count: a program that leaves them out, or rounds other values in their place, can miss the bound.
Values may be sent and summed in bfloat16 or wider, within the bound.
No kernel may reach another device: no remote copies, remote signals or barrier semaphores. Data moves between devices by JAX's collectives and lax.ppermute only.
A program may use at most 128 MiB of HBM per device.

v0:
```python
import functools
import math

import jax
import jax.numpy as jnp
from jax import lax
from jax.experimental import pallas as pl
from jax.experimental.pallas import tpu as pltpu
from jax.sharding import Mesh
from jax.sharding import PartitionSpec as P

HEADS = 40
KV_HEADS = 8
HEAD_DIM = 128
SEQ = ("seq_0", "seq_1", "seq_2")
CHIPS = ("seq_0", "seq_1")
CORE = "seq_2"

NORM_EPS = 1e-06
ROPE_BASE = 1000000.0
MASKED = -1e30
F32 = jnp.float32
BF16 = jnp.bfloat16
HALF = HEAD_DIM // 2
GROUP = HEADS // KV_HEADS
KV_HALF = KV_HEADS // 2
Q_HALF = HEADS // 2
BLOCKS = Q_HALF + 2 * KV_HALF

WHOLE = pl.BlockSpec(memory_space=pltpu.VMEM)
SCALARS = pl.BlockSpec(memory_space=pltpu.SMEM)


def kernel_call(body, out_shape, in_specs, scratch=(), name=None):
    many = isinstance(out_shape, (tuple, list))
    return pl.pallas_call(
        body,
        out_shape=out_shape,
        in_specs=in_specs,
        out_specs=[WHOLE] * len(out_shape) if many else WHOLE,
        scratch_shapes=list(scratch),
        name=name,
    )


def swap(parts):
    return lax.all_to_all(parts, CHIPS, 0, 0)


def partner(array):
    return lax.ppermute(array, CORE, [(0, 1), (1, 0)])


def lanes(shape):
    return lax.broadcasted_iota(jnp.int32, shape, len(shape) - 1)


def pick_kernel(vocab_rows, ids, *refs):
    tokens = len(refs) - 2
    blocks, out, rows = refs[:tokens], refs[tokens], refs[tokens + 1]
    chips, _, lane_count = out.shape
    model_width = rows.shape[1]
    width = model_width // chips
    for t in range(tokens):
        place = ids[t]
        inside = (place >= 0) & (place < vocab_rows)
        row = jnp.where(inside, place & 7, -1)
        block = blocks[t][...].astype(F32)
        at = lax.broadcasted_iota(jnp.int32, block.shape, 0)
        rows[t : t + 1, :] = jnp.sum(jnp.where(at == row, block, 0.0), axis=0, keepdims=True)
    values = rows[...]
    square = jnp.mean(values * values, axis=-1, keepdims=True)
    tail = jnp.broadcast_to(square, (tokens, lane_count - width))
    for j in range(chips):
        out[j, :, :width] = rows[:, j * width : (j + 1) * width]
        out[j, :, width:] = tail


def pick(ids, table, chips):
    vocab_rows, model_width = table.shape
    tokens = ids.shape[0]

    def block_of(t, _, places):
        return (jnp.clip(places[t], 0, vocab_rows - 1) // 8, 0)

    return pl.pallas_call(
        functools.partial(pick_kernel, vocab_rows),
        out_shape=jax.ShapeDtypeStruct((chips, tokens, 128), F32),
        grid_spec=pltpu.PrefetchScalarGridSpec(
            num_scalar_prefetch=1,
            grid=(1,),
            in_specs=[
                pl.BlockSpec((8, model_width), functools.partial(block_of, t))
                for t in range(tokens)
            ],
            out_specs=pl.BlockSpec((chips, tokens, 128), lambda _, places: (0, 0, 0)),
            scratch_shapes=[pltpu.VMEM((tokens, model_width), F32)],
        ),
        name="pick",
    )(ids, *([table] * tokens))


def joint_kernel(core, own, other, gain, weights, out, stream_out):
    c = core[0]
    width = gain.shape[1]
    both = own[...] + other[...]
    stream = both[:, :width]
    square = both[:, width : width + 1]
    normed = (stream * lax.rsqrt(square + NORM_EPS) * gain[...]).astype(BF16)
    stream_out[...] = stream
    at = 0
    for first, count in ((0, Q_HALF), (HEADS, KV_HALF), (HEADS + KV_HEADS, KV_HALF)):
        start = pl.multiple_of((first + count * c) * HEAD_DIM, HEAD_DIM)
        product = jnp.dot(
            normed, weights[:, pl.ds(start, count * HEAD_DIM)], preferred_element_type=F32
        )
        for i in range(count):
            out[at + i] = product[:, i * HEAD_DIM : (i + 1) * HEAD_DIM]
        at += count
    out[at:] = jnp.zeros((out.shape[0] - at, *out.shape[1:]), F32)


def rotate_kernel(place, got, bias, cosine, sine, out):
    total = jnp.sum(got[...], axis=0) + bias[pl.ds(place[0], 1), :]
    joint = total.astype(BF16).astype(F32)
    turned = joint * cosine[...] + pltpu.roll(joint, HALF, 1) * sine[...]
    result = jnp.where(place[1] > 0, turned, joint).astype(BF16)
    out[...] = jnp.broadcast_to(result[None], out.shape)


def attend_kernel(info, heads, keys, other_keys, values, other_values, out):
    tokens = heads.shape[1]
    batch, local_len, _ = keys.shape
    rows = GROUP * tokens
    score_scale = 1.0 / math.sqrt(HEAD_DIM)
    token = lax.broadcasted_iota(jnp.int32, (rows, 1), 0) % tokens
    prompt = token % batch
    spot = lax.broadcasted_iota(jnp.int32, (1, local_len), 1)
    fresh = lax.broadcasted_iota(jnp.int32, (1, tokens), 1)
    fresh_valid = (fresh % batch == prompt) & (fresh <= token) & (info[3] > 0)
    contract = (((1,), (1,)), ((), ()))
    lane = lanes((tokens, HEAD_DIM))
    valid = [
        [(spot + info[1 + side] < info[4 + b]) & (prompt == b) for b in range(batch)]
        for side in range(2)
    ]
    for h in range(KV_HALF):
        columns = slice(h * HEAD_DIM, (h + 1) * HEAD_DIM)
        query = heads[h * GROUP : (h + 1) * GROUP].astype(F32).reshape(rows, HEAD_DIM).astype(BF16)
        scores, kept, matching = [], [], []
        for side, (k_ref, v_ref) in enumerate(((keys, values), (other_keys, other_values))):
            for b in range(batch):
                score = lax.dot_general(
                    query, k_ref[b, :, columns], contract, preferred_element_type=F32
                )
                scores.append(jnp.where(valid[side][b], score * score_scale, MASKED))
                kept.append(valid[side][b])
                matching.append(v_ref[b, :, columns])
        score = lax.dot_general(
            query, heads[Q_HALF + h], contract, preferred_element_type=F32
        )
        scores.append(jnp.where(fresh_valid, score * score_scale, MASKED))
        kept.append(fresh_valid)
        matching.append(heads[Q_HALF + KV_HALF + h])
        top = functools.reduce(
            jnp.maximum, [jnp.max(s, axis=-1, keepdims=True) for s in scores]
        )
        total = jnp.zeros((rows, 1), F32)
        summed = jnp.zeros((rows, HEAD_DIM), F32)
        for s, keep, value in zip(scores, kept, matching):
            weight = jnp.where(keep, jnp.exp(s - top), 0.0)
            total += jnp.sum(weight, axis=-1, keepdims=True)
            summed += jnp.dot(weight.astype(BF16), value, preferred_element_type=F32)
        for g in range(GROUP):
            part = slice(g * tokens, (g + 1) * tokens)
            extra = jnp.where(lane == HALF, top[part], total[part])
            both = summed[part]
            at = 2 * (h * GROUP + g)
            out[at] = jnp.where(lane < HALF, both, extra)
            out[at + 1] = jnp.where(lane < HALF, pltpu.roll(both, HALF, 1), extra)
    used = 2 * Q_HALF
    out[used:] = jnp.zeros((out.shape[0] - used, *out.shape[1:]), F32)


def attend(info, heads, keys, other_keys, values, other_values):
    batch, local_len, key_width = keys.shape
    cut = key_width // 2
    whole = pl.BlockSpec(heads.shape, lambda _, i: (0, 0, 0))
    mine = pl.BlockSpec((batch, local_len, cut), lambda _, i: (0, 0, i[0]))
    return pl.pallas_call(
        attend_kernel,
        out_shape=jax.ShapeDtypeStruct(heads.shape, F32),
        grid_spec=pltpu.PrefetchScalarGridSpec(
            num_scalar_prefetch=1,
            grid=(1,),
            in_specs=[whole, mine, mine, mine, mine],
            out_specs=whole,
        ),
        name="attend",
    )(info, heads, keys, other_keys, values, other_values)


def merge_kernel(got, out):
    parts = got[...]
    tops = parts[:, :, HALF : HALF + 1]
    scale = jnp.exp(tops - jnp.max(tops, axis=0, keepdims=True))
    merged = jnp.sum(parts * scale, axis=0)
    total = merged[:, HALF + 1 : HALF + 2]
    result = (merged / jnp.where(total > 0.0, total, 1.0)).astype(BF16)
    out[...] = jnp.broadcast_to(result[None], out.shape)


def project_kernel(core, own, other, weights, stream, attended, mid_out, out):
    c = core[0]
    tokens, width = stream.shape
    lane = lanes((tokens, HEAD_DIM))
    for pieces, start in ((own, c * Q_HALF), (other, (1 - c) * Q_HALF)):
        for i in range(Q_HALF):
            low = pieces[2 * i].astype(F32)
            high = pltpu.roll(pieces[2 * i + 1].astype(F32), HALF, 1)
            column = pl.multiple_of((start + i) * HEAD_DIM, HEAD_DIM)
            attended[:, pl.ds(column, HEAD_DIM)] = jnp.where(lane < HALF, low, high).astype(BF16)
    mid = stream[...] + lax.dot_general(
        attended[...], weights[...], (((1,), (1,)), ((), ())), preferred_element_type=F32
    )
    mid_out[...] = mid
    padded = jnp.concatenate([mid, jnp.zeros((tokens, HEAD_DIM - width), F32)], axis=1)
    out[...] = jnp.broadcast_to(padded[None], out.shape)


def mlp_kernel(got, gain, w_gate, w_up, w_down, out, flat):
    chips, tokens, lane_count = got.shape
    model_width = flat.shape[1]
    width = model_width // chips
    parts = got[...]
    square = jnp.sum(jnp.sum(parts * parts, axis=0), axis=-1, keepdims=True) / model_width
    for j in range(chips):
        flat[:, j * width : (j + 1) * width] = got[j, :, :width]
    normed = (flat[...] * lax.rsqrt(square + NORM_EPS) * gain[...]).astype(BF16)
    gate = jnp.dot(normed, w_gate[...], preferred_element_type=F32)
    upper = jnp.dot(normed, w_up[...], preferred_element_type=F32)
    hidden = (gate / (1.0 + jnp.exp(-gate)) * upper).astype(BF16)
    flat[...] = jnp.dot(hidden, w_down[...], preferred_element_type=F32)
    tail = jnp.zeros((tokens, lane_count - width), F32)
    for j in range(chips):
        out[j, :, :width] = flat[:, j * width : (j + 1) * width]
        out[j, :, width:] = tail


def body(
    token_ids,
    lengths,
    embed_table,
    attn_gain,
    w_qkv,
    qkv_bias,
    cache_keys,
    cache_values,
    w_out,
    mlp_gain,
    w_gate,
    w_up,
    w_down,
):
    c = lax.axis_index(CORE)
    j = lax.axis_index(CHIPS)
    rank = lax.axis_index(SEQ)
    chips = lax.axis_size(CHIPS)
    steps, batch = token_ids.shape
    tokens = steps * batch
    vocab_rows, model_width = embed_table.shape
    local_len = cache_keys.shape[1]
    features = w_qkv.shape[0]
    width = 2 * features
    core = c.reshape(1)
    tile = (chips, tokens, HEAD_DIM)

    other_qkv = partner(w_qkv)
    other_keys = partner(cache_keys)
    other_values = partner(cache_values)
    own_out = w_out.T
    other_out = partner(own_out)
    first = c == 0
    qkv_rows = jnp.concatenate(
        [jnp.where(first, w_qkv, other_qkv), jnp.where(first, other_qkv, w_qkv)], axis=0
    )
    out_rows = jnp.concatenate(
        [jnp.where(first, own_out, other_out), jnp.where(first, other_out, own_out)], axis=0
    )

    local_ids = token_ids.reshape(-1) - rank * vocab_rows
    got = jnp.sum(swap(pick(local_ids, embed_table, chips)), axis=0)
    gain = lax.dynamic_slice_in_dim(attn_gain, j * width, width, 0).astype(F32)[None]
    sent, stream = kernel_call(
        joint_kernel,
        (jax.ShapeDtypeStruct(tile, F32), jax.ShapeDtypeStruct((tokens, width), F32)),
        [SCALARS] + [WHOLE] * 4,
        name="joint",
    )(core, got, partner(got), gain, qkv_rows)

    positions = (lengths[None, :] + jnp.arange(steps, dtype=jnp.int32)[:, None]).reshape(-1)
    frequency = ROPE_BASE ** (-2.0 * jnp.arange(HALF, dtype=F32) / HEAD_DIM)
    angles = positions.astype(F32)[:, None] * frequency
    cosine = jnp.cos(angles)
    sine = jnp.sin(angles)
    cosine = jnp.concatenate([cosine, cosine], axis=1)
    sine = jnp.concatenate([-sine, sine], axis=1)
    head = jnp.where(
        j < Q_HALF,
        Q_HALF * c + j,
        jnp.where(
            j < Q_HALF + KV_HALF,
            HEADS + KV_HALF * c + (j - Q_HALF),
            HEADS + KV_HEADS + KV_HALF * c + (j - Q_HALF - KV_HALF),
        ),
    )
    head = jnp.where(j < BLOCKS, head, 0)
    place = jnp.stack([head, (j < Q_HALF + KV_HALF).astype(jnp.int32)])
    heads = kernel_call(
        rotate_kernel,
        jax.ShapeDtypeStruct(tile, BF16),
        [SCALARS] + [WHOLE] * 4,
        name="rotate",
    )(place, swap(sent), qkv_bias.reshape(-1, HEAD_DIM), cosine, sine)
    heads = swap(heads)

    info = jnp.stack(
        [
            c,
            rank * local_len,
            (rank + 1 - 2 * c) * local_len,
            (j == 0).astype(jnp.int32),
            *[lengths[b] for b in range(batch)],
        ]
    )
    partial = attend(info, heads, cache_keys, other_keys, cache_values, other_values)
    merged = kernel_call(merge_kernel, jax.ShapeDtypeStruct(tile, BF16), [WHOLE], name="merge")(
        swap(partial)
    )
    pieces = swap(merged)

    attended, mid, sent = kernel_call(
        project_kernel,
        (
            jax.ShapeDtypeStruct((tokens, HEADS * HEAD_DIM), BF16),
            jax.ShapeDtypeStruct((tokens, width), F32),
            jax.ShapeDtypeStruct(tile, F32),
        ),
        [SCALARS] + [WHOLE] * 4,
        name="project",
    )(core, pieces, partner(pieces), out_rows, stream)

    down = kernel_call(
        mlp_kernel,
        jax.ShapeDtypeStruct(tile, F32),
        [WHOLE] * 5,
        [pltpu.VMEM((tokens, model_width), F32)],
        name="mlp",
    )(swap(sent), mlp_gain.astype(F32)[None], w_gate, w_up, w_down)
    summed = jnp.sum(swap(down), axis=0)
    summed = mid + (summed + partner(summed))[:, :width]
    mine = jnp.where(first, summed[:, :features], summed[:, features:])
    layer_out = mine.astype(BF16).reshape(steps, batch, features)
    return (attended.reshape(steps, batch, -1), layer_out)


def solution(mesh):
    finer = Mesh(
        mesh.devices.reshape(mesh.shape["parts"], 8, 8, 2), ("parts", "seq_0", "seq_1", "seq_2")
    )
    return jax.shard_map(
        body,
        mesh=finer,
        in_specs=(
            P(None, "parts"),
            P("parts"),
            P(SEQ, None),
            P(),
            P(SEQ, None),
            P(),
            P("parts", SEQ, None),
            P("parts", SEQ, None),
            P(None, SEQ),
            P(),
            P(None, SEQ),
            P(None, SEQ),
            P(SEQ, None),
        ),
        out_specs=(P(None, "parts", None), P(None, "parts", SEQ)),
        check_vma=False,
    )
```

profile of v0, /device:TPU:513, one launch (start us, length us, event | category | flops | bytes accessed | tf_op | source)
XLA Modules:
  0.0 187.6 jit_solution(8617950337751389406)
XLA Ops:
  0.6 20.5 %collective-permute-start.1 = (bf16[40,7168]{1,0:T(8,128)(2,1)}, bf16[40,7168]{1,0:T(8,128)(2,1)}, u32[]{:S(2)}, u32[]{:S(2)}) collective-permute-start(bf16[40,7168]{1,0:T(8,128)(2,1)} %param.17), channel_id=1, source_target_pairs={{0,1},{1,0},{2,3},{3,2},{4,5},{5,4},{6,7},{7,6},{8,9},{9,8},{10,11... | collective-permute-start | bytes 1720328 | tf_op jit(solution)/shard_map/ppermute | solution.py:51
  21.2 0.7 broadcast_subtract_fusion
  21.8 0.1 copy.16
  21.9 0.6 sub.23.ids
  22.5 3.3 %pick.1 = f32[64,8,128]{2,1,0:T(8,128)} custom-call(s32[8]{0:T(128)} %sub.23.ids, bf16[594,5120]{1,0:T(8,128)(2,1)} %refs_7_.1, bf16[594,5120]{1,0:T(8,128)(2,1)} %refs_7_.1, bf16[594,5120]{1,0:T(8,128)(2,1)} %refs_7_.1, bf16[594,5120]{1,0:T(8,128)(2,1)} %refs_7_.1, bf16[594,5120]{1,0:T(8,128)(2,1)} %refs_7_.1, bf16[594,5120]{1,0:T(8,128)(2,1)} %refs_7_.1, ...), custom_call_target="tpu_custom_call" | custom-call | tf_op jit(solution)/shard_map/pick/pallas_call | solution.py:86
  25.8 6.5 %all-to-all-start = ((f32[64,8,128]{2,1,0:T(8,128)}), f32[64,8,128]{2,1,0:T(8,128)S(1)}, u32[]{:S(2)}, u32[]{:S(2)}) async-start(f32[64,8,128]{2,1,0:T(8,128)} %pick.1), calls=%async_computation | async-start | bytes 524288 | tf_op jit(solution)/shard_map/all_to_all | solution.py:47
  32.3 0.0 copy-done
  32.3 0.2 collective-permute-start.2
  32.5 0.0 copy-done.1
  32.5 0.5 collective-permute-start.3
  33.0 0.0 copy-done.15
  33.0 0.1 convert_element_type.18
  33.1 1.3 bitcast_convert_fusion.gain
  34.4 10.2 %all-to-all-done = f32[64,8,128]{2,1,0:T(8,128)S(1)} async-done(((f32[64,8,128]{2,1,0:T(8,128)}), f32[64,8,128]{2,1,0:T(8,128)S(1)}, u32[]{:S(2)}, u32[]{:S(2)}) %all-to-all-start) | async-done | bytes 262176 | tf_op jit(solution)/shard_map/all_to_all | solution.py:47
  44.6 0.1 reduce_sum.18.own
  44.7 2.1 %collective-permute-start = (f32[8,128]{1,0:T(8,128)S(1)}, f32[8,128]{1,0:T(8,128)S(1)}, u32[]{:S(2)}, u32[]{:S(2)}) collective-permute-start(f32[8,128]{1,0:T(8,128)S(1)} %reduce_sum.18.own), channel_id=1, source_target_pairs={{0,1},{1,0},{2,3},{3,2},{4,5},{5,4},{6,7},{7,6},{8,9},{9,8},{10,11... | collective-permute-start | bytes 12296 | tf_op jit(solution)/shard_map/ppermute | solution.py:51
  46.7 0.0 collective-permute-done.1
  46.8 1.3 broadcast_select_fusion.1
  48.1 1.1 pad_maximum_fusion.weights
  49.2 0.0 collective-permute-done.other
  49.2 0.6 copy-done.13
  49.8 2.3 %joint.1 = (f32[64,8,128]{2,1,0:T(8,128)}, f32[8,80]{1,0:T(8,128)}) custom-call(s32[1]{0:T(128)} %bitcast.core, f32[8,128]{1,0:T(8,128)} %copy-done.11, f32[8,128]{1,0:T(8,128)} %copy-done.13, f32[1,80]{1,0:T(1,128)} %bitcast_convert_fusion.gain, bf16[80,7168]{1,0:T(8,128)(2,1)} %pad_maximum_fusion.weights), custom_call_target="tpu_custom_call" | custom-call | tf_op jit(solution)/shard_map/joint/pallas_call | solution.py:294
  52.0 6.5 %all-to-all-start.1 = ((f32[64,8,128]{2,1,0:T(8,128)}), f32[64,8,128]{2,1,0:T(8,128)S(1)}, u32[]{:S(2)}, u32[]{:S(2)}) async-start(f32[64,8,128]{2,1,0:T(8,128)} %get-tuple-element.7), calls=%async_computation.1 | async-start | bytes 524288 | tf_op jit(solution)/shard_map/all_to_all | solution.py:47
  58.5 0.7 pad_add_fusion.place
  59.2 0.1 fusion
  59.3 0.7 pad_maximum_fusion.2
  60.0 10.8 %all-to-all-done.1.got = f32[64,8,128]{2,1,0:T(8,128)S(1)} async-done(((f32[64,8,128]{2,1,0:T(8,128)}), f32[64,8,128]{2,1,0:T(8,128)S(1)}, u32[]{:S(2)}, u32[]{:S(2)}) %all-to-all-start.1) | async-done | bytes 262176 | tf_op jit(solution)/shard_map/all_to_all | solution.py:47
  70.8 0.7 copy-done.4
  71.5 1.8 rotate.1
  73.3 6.8 %all-to-all-start.2 = ((bf16[64,8,128]{2,1,0:T(8,128)(2,1)}), bf16[64,8,128]{2,1,0:T(8,128)(2,1)S(1)}, u32[]{:S(2)}, u32[]{:S(2)}) async-start(bf16[64,8,128]{2,1,0:T(8,128)(2,1)} %rotate.1), calls=%async_computation.2 | async-start | bytes 262144 | tf_op jit(solution)/shard_map/all_to_all | solution.py:47
  80.1 0.6 stack.32.info
  80.7 0.0 collective-permute-done.2.other_keys
  80.7 0.0 collective-permute-done.3.other_values
  80.7 9.6 %all-to-all-done.2.heads = bf16[64,8,128]{2,1,0:T(8,128)(2,1)S(1)} async-done(((bf16[64,8,128]{2,1,0:T(8,128)(2,1)}), bf16[64,8,128]{2,1,0:T(8,128)(2,1)S(1)}, u32[]{:S(2)}, u32[]{:S(2)}) %all-to-all-start.2) | async-done | bytes 131104 | tf_op jit(solution)/shard_map/all_to_all | solution.py:47
  90.3 0.6 copy-done.6
  91.0 4.5 %attend.1 = f32[64,8,128]{2,1,0:T(8,128)} custom-call(s32[6]{0:T(128)} %stack.32.info, bf16[64,8,128]{2,1,0:T(8,128)(2,1)} %copy-done.6, bf16[2,256,1024]{2,1,0:T(8,128)(2,1)} %keys.1, bf16[2,256,1024]{2,1,0:T(8,128)(2,1)} %copy-done.2, bf16[2,256,1024]{2,1,0:T(8,128)(2,1)} %values.1, bf16[2,256,1024]{2,1,0:T(8,128)(2,1)} %collective-permute-done.3.other_values), custom_call_target="tpu_custom_call" | custom-call | tf_op jit(solution)/shard_map/attend/pallas_call | solution.py:190
  95.4 6.5 %all-to-all-start.3 = ((f32[64,8,128]{2,1,0:T(8,128)}), f32[64,8,128]{2,1,0:T(8,128)S(1)}, u32[]{:S(2)}, u32[]{:S(2)}) async-start(f32[64,8,128]{2,1,0:T(8,128)} %attend.1), calls=%async_computation.3 | async-start | bytes 524288 | tf_op jit(solution)/shard_map/all_to_all | solution.py:47
  101.9 3.0 %collective-permute-start.5 = (bf16[40,5120]{1,0:T(8,128)(2,1)S(1)}, bf16[40,5120]{1,0:T(8,128)(2,1)S(1)}, u32[]{:S(2)}, u32[]{:S(2)}) collective-permute-start(bf16[40,5120]{1,0:T(8,128)(2,1)S(1)} %bitcast.15), channel_id=1, source_target_pairs={{0,1},{1,0},{2,3},{3,2},{4,5},{5,4},{6,7},{7,6},{8,9},{9,8},{10,11... | collective-permute-start | bytes 1228808 | tf_op jit(solution)/shard_map/ppermute | solution.py:51
  105.0 8.2 %all-to-all-done.3.got = f32[64,8,128]{2,1,0:T(8,128)S(1)} async-done(((f32[64,8,128]{2,1,0:T(8,128)}), f32[64,8,128]{2,1,0:T(8,128)S(1)}, u32[]{:S(2)}, u32[]{:S(2)}) %all-to-all-start.3) | async-done | bytes 262176 | tf_op jit(solution)/shard_map/all_to_all | solution.py:47
  113.2 0.7 copy-done.5
  113.9 1.8 merge.1
  115.7 6.5 %all-to-all-start.4 = ((bf16[64,8,128]{2,1,0:T(8,128)(2,1)}), bf16[64,8,128]{2,1,0:T(8,128)(2,1)S(1)}, u32[]{:S(2)}, u32[]{:S(2)}) async-start(bf16[64,8,128]{2,1,0:T(8,128)(2,1)} %merge.1), calls=%async_computation.4 | async-start | bytes 262144 | tf_op jit(solution)/shard_map/all_to_all | solution.py:47
  122.2 0.0 collective-permute-done.5
  122.2 0.1 broadcast_select_fusion.3
  122.3 0.0 copy-start.12
  122.3 10.2 %all-to-all-done.4.own = bf16[64,8,128]{2,1,0:T(8,128)(2,1)S(1)} async-done(((bf16[64,8,128]{2,1,0:T(8,128)(2,1)}), bf16[64,8,128]{2,1,0:T(8,128)(2,1)S(1)}, u32[]{:S(2)}, u32[]{:S(2)}) %all-to-all-start.4) | async-done | bytes 131104 | tf_op jit(solution)/shard_map/all_to_all | solution.py:47
  132.4 4.7 %collective-permute-start.4 = (bf16[64,8,128]{2,1,0:T(8,128)(2,1)S(1)}, bf16[64,8,128]{2,1,0:T(8,128)(2,1)S(1)}, u32[]{:S(2)}, u32[]{:S(2)}) collective-permute-start(bf16[64,8,128]{2,1,0:T(8,128)(2,1)S(1)} %all-to-all-done.4.own), channel_id=1, source_target_pairs={{0,1},{1,0},{2,3},{3,2},{4,5},{5,4},{6,7},{7,6},{8,9},{9,8},{10,11... | collective-permute-start | bytes 393224 | tf_op jit(solution)/shard_map/ppermute | solution.py:51
  137.2 0.9 pad_maximum_fusion.1.weights
  138.1 0.0 collective-permute-done.4.other
  138.2 0.0 copy-done.7
  138.2 0.6 copy-done.9
  138.8 2.4 %project.1 = (bf16[8,5120]{1,0:T(8,128)(2,1)}, f32[8,80]{1,0:T(8,128)}, f32[64,8,128]{2,1,0:T(8,128)}) custom-call(s32[1]{0:T(128)} %bitcast.core, bf16[64,8,128]{2,1,0:T(8,128)(2,1)} %copy-done.7, bf16[64,8,128]{2,1,0:T(8,128)(2,1)} %copy-done.9, bf16[80,5120]{1,0:T(8,128)(2,1)} %pad_maximum_fusion.1.weights, f32[8,80]{1,0:T(8,128)} %get-tuple-element.8.stream), custom_call_target="tpu_custom_call" | custom-call | tf_op jit(solution)/shard_map/project/pallas_call | solution.py:342
  141.2 6.5 %all-to-all-start.5 = ((f32[64,8,128]{2,1,0:T(8,128)}), f32[64,8,128]{2,1,0:T(8,128)S(1)}, u32[]{:S(2)}, u32[]{:S(2)}) async-start(f32[64,8,128]{2,1,0:T(8,128)} %get-tuple-element.11), calls=%async_computation.5 | async-start | bytes 524288 | tf_op jit(solution)/shard_map/all_to_all | solution.py:47
  147.7 0.6 broadcast_in_dim.19
  148.3 11.2 %all-to-all-done.5.got = f32[64,8,128]{2,1,0:T(8,128)S(1)} async-done(((f32[64,8,128]{2,1,0:T(8,128)}), f32[64,8,128]{2,1,0:T(8,128)S(1)}, u32[]{:S(2)}, u32[]{:S(2)}) %all-to-all-start.5) | async-done | bytes 262176 | tf_op jit(solution)/shard_map/all_to_all | solution.py:47
  159.6 0.7 copy-done.3
  160.3 3.9 %mlp.1 = f32[64,8,128]{2,1,0:T(8,128)} custom-call(f32[64,8,128]{2,1,0:T(8,128)} %copy-done.3, f32[1,5120]{1,0:T(1,128)} %bitcast.16, bf16[5120,128]{1,0:T(8,128)(2,1)} %w_gate.1, bf16[5120,128]{1,0:T(8,128)(2,1)} %w_up.1, bf16[128,5120]{1,0:T(8,128)(2,1)} %w_down.1), custom_call_target="tpu_custom_call" | custom-call | tf_op jit(solution)/shard_map/mlp/pallas_call | solution.py:353
  164.2 18.1 %all_to_all.35 = f32[64,8,128]{2,1,0:T(8,128)S(1)} all-to-all(f32[64,8,128]{2,1,0:T(8,128)} %mlp.1), channel_id=1, replica_groups=mesh['parts'=2,'seq_0'=8,'seq_1'=8,'seq_2'=2] {'seq_0','seq_1'}, dimensions={0} | all-to-all | bytes 524288 | tf_op jit(solution)/shard_map/all_to_all | solution.py:47
  182.3 0.1 reduce_sum.19
  182.4 3.8 %collective-permute-start.6 = (f32[8,128]{1,0:T(8,128)S(1)}, f32[8,128]{1,0:T(8,128)S(1)}, u32[]{:S(2)}, u32[]{:S(2)}) collective-permute-start(f32[8,128]{1,0:T(8,128)S(1)} %reduce_sum.19), channel_id=1, source_target_pairs={{0,1},{1,0},{2,3},{3,2},{4,5},{5,4},{6,7},{7,6},{8,9},{9,8},{10,11... | collective-permute-start | bytes 12296 | tf_op jit(solution)/shard_map/ppermute | solution.py:51
  186.1 0.0 copy-done.10
  186.1 0.7 reshape.42
  186.8 0.2 collective-permute-done.6
  187.0 0.7 select_convert_fusion
  (24 shorter events, 0.1 us)
Async XLA Ops:
  0.6 46.1 %collective-permute-start.1 = (bf16[40,7168]{1,0:T(8,128)(2,1)}, bf16[40,7168]{1,0:T(8,128)(2,1)}, u32[]{:S(2)}, u32[]{:S(2)}) collective-permute-start(bf16[40,7168]{1,0:T(8,128)(2,1)} %param.17), channel_id=1, source_target_pairs={{0,1},{1,0},{2,3},{3,2},{4,5},{5,4},{6,7},{7,6},{8,9},{9,8},{10,11... | collective-permute-start | bytes 1720328 | tf_op jit(solution)/shard_map/ppermute | solution.py:51
  22.5 9.8 %copy-start = (bf16[2,256,1024]{2,1,0:T(8,128)(2,1)S(1)}, bf16[2,256,1024]{2,1,0:T(8,128)(2,1)}, u32[]{:S(2)}) copy-start(bf16[2,256,1024]{2,1,0:T(8,128)(2,1)} %keys.1) | copy-start | bytes 3145732
  22.5 10.0 %copy-start.1 = (bf16[2,256,1024]{2,1,0:T(8,128)(2,1)S(1)}, bf16[2,256,1024]{2,1,0:T(8,128)(2,1)}, u32[]{:S(2)}) copy-start(bf16[2,256,1024]{2,1,0:T(8,128)(2,1)} %values.1) | copy-start | bytes 3145732
  22.5 10.4 %copy-start.15 = (s32[2]{0:T(128)S(1)}, s32[2]{0:T(128)}, u32[]{:S(2)}) copy-start(s32[2]{0:T(128)} %param.14) | copy-start | bytes 28
  25.8 18.7 %all-to-all-start = ((f32[64,8,128]{2,1,0:T(8,128)}), f32[64,8,128]{2,1,0:T(8,128)S(1)}, u32[]{:S(2)}, u32[]{:S(2)}) async-start(f32[64,8,128]{2,1,0:T(8,128)} %pick.1), calls=%async_computation | async-start | bytes 524288 | tf_op jit(solution)/shard_map/all_to_all | solution.py:47
  32.3 48.3 %collective-permute-start.2 = (bf16[2,256,1024]{2,1,0:T(8,128)(2,1)S(1)}, bf16[2,256,1024]{2,1,0:T(8,128)(2,1)S(1)}, u32[]{:S(2)}, u32[]{:S(2)}) collective-permute-start(bf16[2,256,1024]{2,1,0:T(8,128)(2,1)S(1)} %copy-done), channel_id=1, source_target_pairs={{0,1},{1,0},{2,3},{3,2},{4,5},{5,4},{6,7},{7,6},{8,9},{9,8},{10,11... | collective-permute-start | bytes 3145736 | tf_op jit(solution)/shard_map/ppermute | solution.py:51
  32.5 48.2 %collective-permute-start.3 = (bf16[2,256,1024]{2,1,0:T(8,128)(2,1)S(1)}, bf16[2,256,1024]{2,1,0:T(8,128)(2,1)}, u32[]{:S(2)}, u32[]{:S(2)}) collective-permute-start(bf16[2,256,1024]{2,1,0:T(8,128)(2,1)S(1)} %copy-done.1), channel_id=1, source_target_pairs={{0,1},{1,0},{2,3},{3,2},{4,5},{5,4},{6,7},{7,6},{8,9},{9,8},{10,11... | collective-permute-start | bytes 3145736 | tf_op jit(solution)/shard_map/ppermute | solution.py:51
  44.7 4.5 %copy-start.11 = (f32[8,128]{1,0:T(8,128)}, f32[8,128]{1,0:T(8,128)S(1)}, u32[]{:S(2)}) copy-start(f32[8,128]{1,0:T(8,128)S(1)} %reduce_sum.18.own) | copy-start | bytes 12292
  44.7 4.5 %collective-permute-start = (f32[8,128]{1,0:T(8,128)S(1)}, f32[8,128]{1,0:T(8,128)S(1)}, u32[]{:S(2)}, u32[]{:S(2)}) collective-permute-start(f32[8,128]{1,0:T(8,128)S(1)} %reduce_sum.18.own), channel_id=1, source_target_pairs={{0,1},{1,0},{2,3},{3,2},{4,5},{5,4},{6,7},{7,6},{8,9},{9,8},{10,11... | collective-permute-start | bytes 12296 | tf_op jit(solution)/shard_map/ppermute | solution.py:51
  49.2 0.6 copy-start.13
  52.0 18.8 %all-to-all-start.1 = ((f32[64,8,128]{2,1,0:T(8,128)}), f32[64,8,128]{2,1,0:T(8,128)S(1)}, u32[]{:S(2)}, u32[]{:S(2)}) async-start(f32[64,8,128]{2,1,0:T(8,128)} %get-tuple-element.7), calls=%async_computation.1 | async-start | bytes 524288 | tf_op jit(solution)/shard_map/all_to_all | solution.py:47
  70.8 0.7 copy-start.4
  73.3 17.0 %all-to-all-start.2 = ((bf16[64,8,128]{2,1,0:T(8,128)(2,1)}), bf16[64,8,128]{2,1,0:T(8,128)(2,1)S(1)}, u32[]{:S(2)}, u32[]{:S(2)}) async-start(bf16[64,8,128]{2,1,0:T(8,128)(2,1)} %rotate.1), calls=%async_computation.2 | async-start | bytes 262144 | tf_op jit(solution)/shard_map/all_to_all | solution.py:47
  80.7 9.6 %copy-start.2 = (bf16[2,256,1024]{2,1,0:T(8,128)(2,1)}, bf16[2,256,1024]{2,1,0:T(8,128)(2,1)S(1)}, u32[]{:S(2)}) copy-start(bf16[2,256,1024]{2,1,0:T(8,128)(2,1)S(1)} %collective-permute-done.2.other_keys) | copy-start | bytes 3145732
  80.7 21.2 %copy-start.8 = (bf16[5120,40]{0,1:T(8,128)(2,1)S(1)}, bf16[5120,40]{0,1:T(8,128)(2,1)}, u32[]{:S(2)}) copy-start(bf16[5120,40]{0,1:T(8,128)(2,1)} %param.21) | copy-start | bytes 1228804
  90.3 0.7 copy-start.6
  95.4 17.8 %all-to-all-start.3 = ((f32[64,8,128]{2,1,0:T(8,128)}), f32[64,8,128]{2,1,0:T(8,128)S(1)}, u32[]{:S(2)}, u32[]{:S(2)}) async-start(f32[64,8,128]{2,1,0:T(8,128)} %attend.1), calls=%async_computation.3 | async-start | bytes 524288 | tf_op jit(solution)/shard_map/all_to_all | solution.py:47
  101.9 20.3 %collective-permute-start.5 = (bf16[40,5120]{1,0:T(8,128)(2,1)S(1)}, bf16[40,5120]{1,0:T(8,128)(2,1)S(1)}, u32[]{:S(2)}, u32[]{:S(2)}) collective-permute-start(bf16[40,5120]{1,0:T(8,128)(2,1)S(1)} %bitcast.15), channel_id=1, source_target_pairs={{0,1},{1,0},{2,3},{3,2},{4,5},{5,4},{6,7},{7,6},{8,9},{9,8},{10,11... | collective-permute-start | bytes 1228808 | tf_op jit(solution)/shard_map/ppermute | solution.py:51
  113.2 0.7 copy-start.5
  115.7 16.7 %all-to-all-start.4 = ((bf16[64,8,128]{2,1,0:T(8,128)(2,1)}), bf16[64,8,128]{2,1,0:T(8,128)(2,1)S(1)}, u32[]{:S(2)}, u32[]{:S(2)}) async-start(bf16[64,8,128]{2,1,0:T(8,128)(2,1)} %merge.1), calls=%async_computation.4 | async-start | bytes 262144 | tf_op jit(solution)/shard_map/all_to_all | solution.py:47
  122.3 25.5 %copy-start.12 = (bf16[5120]{0:T(1024)(128)(2,1)S(1)}, bf16[5120]{0:T(1024)(128)(2,1)}, u32[]{:S(2)}) copy-start(bf16[5120]{0:T(1024)(128)(2,1)} %param.22) | copy-start | bytes 30724
  132.4 5.7 %copy-start.7 = (bf16[64,8,128]{2,1,0:T(8,128)(2,1)}, bf16[64,8,128]{2,1,0:T(8,128)(2,1)S(1)}, u32[]{:S(2)}) copy-start(bf16[64,8,128]{2,1,0:T(8,128)(2,1)S(1)} %all-to-all-done.4.own) | copy-start | bytes 393220
  132.4 5.7 %collective-permute-start.4 = (bf16[64,8,128]{2,1,0:T(8,128)(2,1)S(1)}, bf16[64,8,128]{2,1,0:T(8,128)(2,1)S(1)}, u32[]{:S(2)}, u32[]{:S(2)}) collective-permute-start(bf16[64,8,128]{2,1,0:T(8,128)(2,1)S(1)} %all-to-all-done.4.own), channel_id=1, source_target_pairs={{0,1},{1,0},{2,3},{3,2},{4,5},{5,4},{6,7},{7,6},{8,9},{9,8},{10,11... | collective-permute-start | bytes 393224 | tf_op jit(solution)/shard_map/ppermute | solution.py:51
  138.2 0.6 copy-start.9
  141.2 18.3 %all-to-all-start.5 = ((f32[64,8,128]{2,1,0:T(8,128)}), f32[64,8,128]{2,1,0:T(8,128)S(1)}, u32[]{:S(2)}, u32[]{:S(2)}) async-start(f32[64,8,128]{2,1,0:T(8,128)} %get-tuple-element.11), calls=%async_computation.5 | async-start | bytes 524288 | tf_op jit(solution)/shard_map/all_to_all | solution.py:47
  159.6 0.7 copy-start.3
  160.3 25.9 %copy-start.10 = (bf16[8,5120]{1,0:T(8,128)(2,1)S(1)}, bf16[8,5120]{1,0:T(8,128)(2,1)}, u32[]{:S(2)}) copy-start(bf16[8,5120]{1,0:T(8,128)(2,1)} %get-tuple-element.9) | copy-start | bytes 245764
  160.3 26.7 %copy-start.14 = (f32[8,80]{1,0:T(8,128)S(1)}, f32[8,80]{1,0:T(8,128)}, u32[]{:S(2)}) copy-start(f32[8,80]{1,0:T(8,128)} %get-tuple-element.10) | copy-start | bytes 7684
  182.4 4.6 %collective-permute-start.6 = (f32[8,128]{1,0:T(8,128)S(1)}, f32[8,128]{1,0:T(8,128)S(1)}, u32[]{:S(2)}, u32[]{:S(2)}) collective-permute-start(f32[8,128]{1,0:T(8,128)S(1)} %reduce_sum.19), channel_id=1, source_target_pairs={{0,1},{1,0},{2,3},{3,2},{4,5},{5,4},{6,7},{7,6},{8,9},{9,8},{10,11... | collective-permute-start | bytes 12296 | tf_op jit(solution)/shard_map/ppermute | solution.py:51
where the time goes:
time: 188 us
  starting transfers between devices  74 us (39%)
  waiting for transfers between devices  60.5 us (32%)
  Pallas kernels  20 us (11%)
  blocking collectives  18.1 us (10%)
  other arithmetic  8.31 us (4%)
  local copies, waits for them, and re-layouts  6.01 us (3%)
    all_to_all x6, waiting for transfers between devices, swap(): return lax.all_to_all(parts, CHIPS, 0, 0)  60.3 us
    all_to_all x6, starting transfers between devices, swap(): return lax.all_to_all(parts, CHIPS, 0, 0)  39.2 us
    ppermute x7, starting transfers between devices, partner(): return lax.ppermute(array, CORE, [(0, 1), (1, 0)])  34.8 us
    all_to_all x1, blocking collectives, swap(): return lax.all_to_all(parts, CHIPS, 0, 0)  18.1 us
    pallas_call x1, Pallas kernels, attend(): pl.pallas_call(attend_kernel, out_shape=jax.ShapeDtypeStruct(heads.shape,...  4.47 us
    unnamed x32, local copies, waits for them, and re-layouts  3.99 us
    pallas_call x1, Pallas kernels, body(): kernel_call(mlp_kernel, jax.ShapeDtypeStruct(tile, F32), [WHOLE] * 5, [pl...  3.88 us
  transfers between devices with their start and end apart: 13, of which 7 were waited for; matrix products, arithmetic and copies ran while one was open for 5% of the time, Pallas kernels for 5%

commit v1 on v0

--- a/solution.py
+++ b/solution.py
@@ -29,9 +29,14 @@
 
 WHOLE = pl.BlockSpec(memory_space=pltpu.VMEM)
 SCALARS = pl.BlockSpec(memory_space=pltpu.SMEM)
-
-
-def kernel_call(body, out_shape, in_specs, scratch=(), name=None):
+STAYS = pl.BlockSpec(memory_space=pltpu.HBM)
+
+
+def grant(mebibytes):
+    return pltpu.CompilerParams(vmem_limit_bytes=mebibytes * 1024 * 1024)
+
+
+def kernel_call(body, out_shape, in_specs, scratch=(), name=None, room=12):
     many = isinstance(out_shape, (tuple, list))
     return pl.pallas_call(
         body,
@@ -39,6 +44,7 @@
         in_specs=in_specs,
         out_specs=[WHOLE] * len(out_shape) if many else WHOLE,
         scratch_shapes=list(scratch),
+        compiler_params=grant(room),
         name=name,
     )
 
@@ -55,73 +61,107 @@
     return lax.broadcasted_iota(jnp.int32, shape, len(shape) - 1)
 
 
-def pick_kernel(vocab_rows, ids, *refs):
+def in_pieces(value):
+    high = value.astype(BF16).astype(F32)
+    rest = value - high
+    middle = rest.astype(BF16).astype(F32)
+    return high, middle, rest - middle
+
+
+def own_first(core, left, right):
+    return jnp.where(core == 0, left, right), jnp.where(core == 0, right, left)
+
+
+def pick_kernel(vocab_rows, rank, ids, *refs):
     tokens = len(refs) - 2
+    batch = ids.shape[0]
     blocks, out, rows = refs[:tokens], refs[tokens], refs[tokens + 1]
     chips, _, lane_count = out.shape
     model_width = rows.shape[1]
     width = model_width // chips
     for t in range(tokens):
-        place = ids[t]
+        place = ids[t % batch, t // batch] - rank[0] * vocab_rows
         inside = (place >= 0) & (place < vocab_rows)
         row = jnp.where(inside, place & 7, -1)
         block = blocks[t][...].astype(F32)
         at = lax.broadcasted_iota(jnp.int32, block.shape, 0)
         rows[t : t + 1, :] = jnp.sum(jnp.where(at == row, block, 0.0), axis=0, keepdims=True)
     values = rows[...]
-    square = jnp.mean(values * values, axis=-1, keepdims=True)
-    tail = jnp.broadcast_to(square, (tokens, lane_count - width))
+    square = in_pieces(jnp.mean(values * values, axis=-1, keepdims=True))
+    lane = lanes((tokens, lane_count - width))
+    tail = jnp.zeros(lane.shape, F32)
+    for i, piece in enumerate(square):
+        tail = jnp.where(lane == i, piece, tail)
     for j in range(chips):
-        out[j, :, :width] = rows[:, j * width : (j + 1) * width]
-        out[j, :, width:] = tail
-
-
-def pick(ids, table, chips):
+        both = jnp.concatenate([rows[:, j * width : (j + 1) * width], tail], axis=1)
+        out[j] = both.astype(BF16)
+
+
+def pick(rank, ids, table, chips):
     vocab_rows, model_width = table.shape
-    tokens = ids.shape[0]
-
-    def block_of(t, _, places):
-        return (jnp.clip(places[t], 0, vocab_rows - 1) // 8, 0)
+    batch, steps = ids.shape
+    tokens = steps * batch
+
+    def block_of(t, _, number, places):
+        place = places[t % batch, t // batch] - number[0] * vocab_rows
+        return (jnp.clip(place, 0, vocab_rows - 1) // 8, 0)
 
     return pl.pallas_call(
         functools.partial(pick_kernel, vocab_rows),
-        out_shape=jax.ShapeDtypeStruct((chips, tokens, 128), F32),
+        out_shape=jax.ShapeDtypeStruct((chips, tokens, 128), BF16),
         grid_spec=pltpu.PrefetchScalarGridSpec(
-            num_scalar_prefetch=1,
+            num_scalar_prefetch=2,
             grid=(1,),
             in_specs=[
                 pl.BlockSpec((8, model_width), functools.partial(block_of, t))
                 for t in range(tokens)
             ],
-            out_specs=pl.BlockSpec((chips, tokens, 128), lambda _, places: (0, 0, 0)),
+            out_specs=pl.BlockSpec((chips, tokens, 128), lambda _, number, places: (0, 0, 0)),
             scratch_shapes=[pltpu.VMEM((tokens, model_width), F32)],
         ),
+        compiler_params=grant(50),
         name="pick",
-    )(ids, *([table] * tokens))
-
-
-def joint_kernel(core, own, other, gain, weights, out, stream_out):
+    )(rank, ids, *([table] * tokens))
+
+
+def joint_kernel(
+    core, own, other, gain, weights, other_weights, out, stream_out, held, other_held, sems
+):
     c = core[0]
+    groups = ((0, Q_HALF), (HEADS, KV_HALF), (HEADS + KV_HEADS, KV_HALF))
+    copies, at = [], 0
+    for n, (first, count) in enumerate(groups):
+        start = pl.multiple_of((first + count * c) * HEAD_DIM, HEAD_DIM)
+        columns = pl.ds(start, count * HEAD_DIM)
+        places = pl.ds(at * HEAD_DIM, count * HEAD_DIM)
+        for side, (source, target) in enumerate(((weights, held), (other_weights, other_held))):
+            copy = pltpu.make_async_copy(
+                source.at[:, columns], target.at[:, places], sems.at[n, side]
+            )
+            copy.start()
+            copies.append(copy)
+        at += count
     width = gain.shape[1]
+    features = width // 2
     both = own[...] + other[...]
     stream = both[:, :width]
-    square = both[:, width : width + 1]
-    normed = (stream * lax.rsqrt(square + NORM_EPS) * gain[...]).astype(BF16)
+    square = jnp.sum(both[:, width : width + 3], axis=-1, keepdims=True)
+    normed = (stream * lax.rsqrt(square + NORM_EPS) * gain[...]).astype(BF16).astype(F32)
     stream_out[...] = stream
-    at = 0
-    for first, count in ((0, Q_HALF), (HEADS, KV_HALF), (HEADS + KV_HEADS, KV_HALF)):
-        start = pl.multiple_of((first + count * c) * HEAD_DIM, HEAD_DIM)
-        product = jnp.dot(
-            normed, weights[:, pl.ds(start, count * HEAD_DIM)], preferred_element_type=F32
-        )
-        for i in range(count):
-            out[at + i] = product[:, i * HEAD_DIM : (i + 1) * HEAD_DIM]
-        at += count
-    out[at:] = jnp.zeros((out.shape[0] - at, *out.shape[1:]), F32)
+    mine, others = own_first(c, normed[:, :features], normed[:, features:])
+    mine, others = mine.astype(BF16), others.astype(BF16)
+    out[BLOCKS:] = jnp.zeros((out.shape[0] - BLOCKS, *out.shape[1:]), BF16)
+    for copy in copies:
+        copy.wait()
+    product = jnp.dot(mine, held[...], preferred_element_type=F32)
+    product += jnp.dot(others, other_held[...], preferred_element_type=F32)
+    product = product.astype(BF16)
+    for i in range(BLOCKS):
+        out[i] = product[:, i * HEAD_DIM : (i + 1) * HEAD_DIM]
 
 
 def rotate_kernel(place, got, bias, cosine, sine, out):
-    total = jnp.sum(got[...], axis=0) + bias[pl.ds(place[0], 1), :]
+    total = jnp.sum(got[...].astype(F32), axis=0) + bias[pl.ds(place[0], 1), :]
     joint = total.astype(BF16).astype(F32)
     turned = joint * cosine[...] + pltpu.roll(joint, HALF, 1) * sine[...]
     result = jnp.where(place[1] > 0, turned, joint).astype(BF16)
@@ -173,13 +213,15 @@
             summed += jnp.dot(weight.astype(BF16), value, preferred_element_type=F32)
         for g in range(GROUP):
             part = slice(g * tokens, (g + 1) * tokens)
-            extra = jnp.where(lane == HALF, top[part], total[part])
+            extra = jnp.zeros(lane.shape, F32)
+            for i, piece in enumerate(in_pieces(top[part]) + in_pieces(total[part])):
+                extra = jnp.where(lane == HALF + i, piece, extra)
             both = summed[part]
             at = 2 * (h * GROUP + g)
-            out[at] = jnp.where(lane < HALF, both, extra)
-            out[at + 1] = jnp.where(lane < HALF, pltpu.roll(both, HALF, 1), extra)
+            out[at] = jnp.where(lane < HALF, both, extra).astype(BF16)
+            out[at + 1] = jnp.where(lane < HALF, pltpu.roll(both, HALF, 1), extra).astype(BF16)
     used = 2 * Q_HALF
-    out[used:] = jnp.zeros((out.shape[0] - used, *out.shape[1:]), F32)
+    out[used:] = jnp.zeros((out.shape[0] - used, *out.shape[1:]), BF16)
 
 
 def attend(info, heads, keys, other_keys, values, other_values):
@@ -189,28 +231,37 @@
     mine = pl.BlockSpec((batch, local_len, cut), lambda _, i: (0, 0, i[0]))
     return pl.pallas_call(
         attend_kernel,
-        out_shape=jax.ShapeDtypeStruct(heads.shape, F32),
+        out_shape=jax.ShapeDtypeStruct(heads.shape, BF16),
         grid_spec=pltpu.PrefetchScalarGridSpec(
             num_scalar_prefetch=1,
             grid=(1,),
             in_specs=[whole, mine, mine, mine, mine],
             out_specs=whole,
         ),
+        compiler_params=grant(53),
         name="attend",
     )(info, heads, keys, other_keys, values, other_values)
 
 
 def merge_kernel(got, out):
-    parts = got[...]
-    tops = parts[:, :, HALF : HALF + 1]
+    parts = got[...].astype(F32)
+    tops = jnp.sum(parts[:, :, HALF : HALF + 3], axis=-1, keepdims=True)
     scale = jnp.exp(tops - jnp.max(tops, axis=0, keepdims=True))
     merged = jnp.sum(parts * scale, axis=0)
-    total = merged[:, HALF + 1 : HALF + 2]
+    total = jnp.sum(merged[:, HALF + 3 : HALF + 6], axis=-1, keepdims=True)
     result = (merged / jnp.where(total > 0.0, total, 1.0)).astype(BF16)
     out[...] = jnp.broadcast_to(result[None], out.shape)
 
 
-def project_kernel(core, own, other, weights, stream, attended, mid_out, out):
+def project_kernel(
+    core, own, other, weights, other_weights, stream, attended, mid_out, out, held, other_held, sems
+):
+    copies = [
+        pltpu.make_async_copy(weights, held, sems.at[0]),
+        pltpu.make_async_copy(other_weights, other_held, sems.at[1]),
+    ]
+    for copy in copies:
+        copy.start()
     c = core[0]
     tokens, width = stream.shape
     lane = lanes((tokens, HEAD_DIM))
@@ -220,31 +271,45 @@
             high = pltpu.roll(pieces[2 * i + 1].astype(F32), HALF, 1)
             column = pl.multiple_of((start + i) * HEAD_DIM, HEAD_DIM)
             attended[:, pl.ds(column, HEAD_DIM)] = jnp.where(lane < HALF, low, high).astype(BF16)
-    mid = stream[...] + lax.dot_general(
-        attended[...], weights[...], (((1,), (1,)), ((), ())), preferred_element_type=F32
-    )
+    rows = attended[...]
+    contract = (((1,), (1,)), ((), ()))
+    for copy in copies:
+        copy.wait()
+    mine = lax.dot_general(rows, held[...], contract, preferred_element_type=F32)
+    others = lax.dot_general(rows, other_held[...], contract, preferred_element_type=F32)
+    mid = stream[...] + jnp.concatenate(own_first(c, mine, others), axis=1)
     mid_out[...] = mid
     padded = jnp.concatenate([mid, jnp.zeros((tokens, HEAD_DIM - width), F32)], axis=1)
-    out[...] = jnp.broadcast_to(padded[None], out.shape)
-
-
-def mlp_kernel(got, gain, w_gate, w_up, w_down, out, flat):
+    out[...] = jnp.broadcast_to(padded.astype(BF16)[None], out.shape)
+
+
+def mlp_kernel(got, gain, w_gate, w_up, w_down, out, flat, gate_held, up_held, down_held, sems):
+    held = (gate_held, up_held, down_held)
+    copies = [
+        pltpu.make_async_copy(source, target, sems.at[n])
+        for n, (source, target) in enumerate(zip((w_gate, w_up, w_down), held))
+    ]
+    for copy in copies:
+        copy.start()
     chips, tokens, lane_count = got.shape
     model_width = flat.shape[1]
     width = model_width // chips
-    parts = got[...]
+    parts = got[...].astype(F32)
     square = jnp.sum(jnp.sum(parts * parts, axis=0), axis=-1, keepdims=True) / model_width
     for j in range(chips):
-        flat[:, j * width : (j + 1) * width] = got[j, :, :width]
+        flat[:, j * width : (j + 1) * width] = parts[j, :, :width]
     normed = (flat[...] * lax.rsqrt(square + NORM_EPS) * gain[...]).astype(BF16)
-    gate = jnp.dot(normed, w_gate[...], preferred_element_type=F32)
-    upper = jnp.dot(normed, w_up[...], preferred_element_type=F32)
+    copies[0].wait()
+    gate = jnp.dot(normed, gate_held[...], preferred_element_type=F32)
+    copies[1].wait()
+    upper = jnp.dot(normed, up_held[...], preferred_element_type=F32)
     hidden = (gate / (1.0 + jnp.exp(-gate)) * upper).astype(BF16)
-    flat[...] = jnp.dot(hidden, w_down[...], preferred_element_type=F32)
+    copies[2].wait()
+    flat[...] = jnp.dot(hidden, down_held[...], preferred_element_type=F32)
     tail = jnp.zeros((tokens, lane_count - width), F32)
     for j in range(chips):
-        out[j, :, :width] = flat[:, j * width : (j + 1) * width]
-        out[j, :, width:] = tail
+        both = jnp.concatenate([flat[:, j * width : (j + 1) * width], tail], axis=1)
+        out[j] = both.astype(BF16)
 
 
 def body(
@@ -268,7 +333,7 @@
     chips = lax.axis_size(CHIPS)
     steps, batch = token_ids.shape
     tokens = steps * batch
-    vocab_rows, model_width = embed_table.shape
+    model_width = embed_table.shape[1]
     local_len = cache_keys.shape[1]
     features = w_qkv.shape[0]
     width = 2 * features
@@ -280,23 +345,17 @@
     other_values = partner(cache_values)
     own_out = w_out.T
     other_out = partner(own_out)
-    first = c == 0
-    qkv_rows = jnp.concatenate(
-        [jnp.where(first, w_qkv, other_qkv), jnp.where(first, other_qkv, w_qkv)], axis=0
-    )
-    out_rows = jnp.concatenate(
-        [jnp.where(first, own_out, other_out), jnp.where(first, other_out, own_out)], axis=0
-    )
-
-    local_ids = token_ids.reshape(-1) - rank * vocab_rows
-    got = jnp.sum(swap(pick(local_ids, embed_table, chips)), axis=0)
+
+    sent = pick(rank.reshape(1), token_ids.T, embed_table, chips)
+    got = jnp.sum(swap(sent).astype(F32), axis=0)
     gain = lax.dynamic_slice_in_dim(attn_gain, j * width, width, 0).astype(F32)[None]
     sent, stream = kernel_call(
         joint_kernel,
-        (jax.ShapeDtypeStruct(tile, F32), jax.ShapeDtypeStruct((tokens, width), F32)),
-        [SCALARS] + [WHOLE] * 4,
+        (jax.ShapeDtypeStruct(tile, BF16), jax.ShapeDtypeStruct((tokens, width), F32)),
+        [SCALARS] + [WHOLE] * 3 + [STAYS] * 2,
+        [pltpu.VMEM((features, BLOCKS * HEAD_DIM), BF16)] * 2 + [pltpu.SemaphoreType.DMA((3, 2))],
         name="joint",
-    )(core, got, partner(got), gain, qkv_rows)
+    )(core, got, partner(got), gain, w_qkv, other_qkv)
 
     positions = (lengths[None, :] + jnp.arange(steps, dtype=jnp.int32)[:, None]).reshape(-1)
     frequency = ROPE_BASE ** (-2.0 * jnp.arange(HALF, dtype=F32) / HEAD_DIM)
@@ -344,22 +403,28 @@
         (
             jax.ShapeDtypeStruct((tokens, HEADS * HEAD_DIM), BF16),
             jax.ShapeDtypeStruct((tokens, width), F32),
-            jax.ShapeDtypeStruct(tile, F32),
+            jax.ShapeDtypeStruct(tile, BF16),
         ),
-        [SCALARS] + [WHOLE] * 4,
+        [SCALARS] + [WHOLE] * 2 + [STAYS] * 2 + [WHOLE],
+        [pltpu.VMEM(own_out.shape, BF16)] * 2 + [pltpu.SemaphoreType.DMA((2,))],
         name="project",
-    )(core, pieces, partner(pieces), out_rows, stream)
+    )(core, pieces, partner(pieces), own_out, other_out, stream)
 
     down = kernel_call(
         mlp_kernel,
-        jax.ShapeDtypeStruct(tile, F32),
-        [WHOLE] * 5,
-        [pltpu.VMEM((tokens, model_width), F32)],
+        jax.ShapeDtypeStruct(tile, BF16),
+        [WHOLE] * 2 + [STAYS] * 3,
+        [
+            pltpu.VMEM((tokens, model_width), F32),
+            *[pltpu.VMEM(weights.shape, BF16) for weights in (w_gate, w_up, w_down)],
+            pltpu.SemaphoreType.DMA((3,)),
+        ],
         name="mlp",
+        room=53,
     )(swap(sent), mlp_gain.astype(F32)[None], w_gate, w_up, w_down)
-    summed = jnp.sum(swap(down), axis=0)
+    summed = jnp.sum(swap(down).astype(F32), axis=0)
     summed = mid + (summed + partner(summed))[:, :width]
-    mine = jnp.where(first, summed[:, :features], summed[:, features:])
+    mine = jnp.where(c == 0, summed[:, :features], summed[:, features:])
     layer_out = mine.astype(BF16).reshape(steps, batch, features)
     return (attended.reshape(steps, batch, -1), layer_out)
 

time: 188 us -> 168 us (0.89)
  blocking collectives: 18.1 us -> 32.8 us
  waiting for transfers between devices: 60.5 us -> 47.8 us
  starting transfers between devices: 74 us -> 67.4 us
  other arithmetic: 8.31 us -> 1.84 us
  Pallas kernels: 20 us -> 14.8 us
  local copies, waits for them, and re-layouts: 6.01 us -> 1.54 us
    all_to_all x1 -> x2, blocking collectives: 18.1 us -> 32.8 us  [swap(): return lax.all_to_all(parts, CHIPS, 0, 0)]
    all_to_all x6 -> x5, waiting for transfers between devices: 60.3 us -> 46.7 us  [swap(): return lax.all_to_all(parts, CHIPS, 0, 0)]
    all_to_all x6 -> x5, starting transfers between devices: 39.2 us -> 32.6 us  [swap(): return lax.all_to_all(parts, CHIPS, 0, 0)]
    unnamed x32 -> x16, local copies, waits for them, and re-layouts: 3.99 us -> 0.7 us
    pallas_call x2, Pallas kernels: 6.13 us -> 3.89 us  [the longest x1 2.51 us: body(): kernel_call(mlp_kernel, jax.ShapeDtypeStruct(tile, BF16), [WHOLE] * 2 + [...]
    concatenate x2 -> x0, other arithmetic: 2.05 us -> none  [the longest x1 1.1 us: body(): jnp.concatenate([jnp.where(first, w_qkv, other_qkv), jnp.where(first, oth...]
  transfers between devices with their start and end apart: 13 -> 12, of which waited for: 7 -> 7; matrix products, arithmetic and copies ran while one was open for 5% -> 1% of each run, Pallas kernels for 5% -> 4%
where the time goes in v1:
time: 168 us; the launch traced here: 167 us
  starting transfers between devices  67.4 us (40%)
  waiting for transfers between devices  47.8 us (28%)
  blocking collectives  32.8 us (20%)
  Pallas kernels  14.8 us (9%)
  other arithmetic  1.84 us (1%)
    all_to_all x5, waiting for transfers between devices, swap(): return lax.all_to_all(parts, CHIPS, 0, 0)  46.7 us
    ppermute x7, starting transfers between devices, partner(): return lax.ppermute(array, CORE, [(0, 1), (1, 0)])  34.8 us
    all_to_all x2, blocking collectives, swap(): return lax.all_to_all(parts, CHIPS, 0, 0)  32.8 us
    all_to_all x5, starting transfers between devices, swap(): return lax.all_to_all(parts, CHIPS, 0, 0)  32.6 us
    pallas_call x1, Pallas kernels, attend(): pl.pallas_call(attend_kernel, out_shape=jax.ShapeDtypeStruct(heads.shape,...  4.22 us
  transfers between devices with their start and end apart: 12, of which 7 were waited for; matrix products, arithmetic and copies ran while one was open for 1% of the time, Pallas kernels for 4%

profile of v1, /device:TPU:513, one launch (start us, length us, event | category | flops | bytes accessed | tf_op | source)
XLA Modules:
  0.0 167.0 jit_solution(5411882459721137627)
XLA Ops:
  0.6 20.5 %collective-permute-start.1 = (bf16[40,7168]{1,0:T(8,128)(2,1)}, bf16[40,7168]{1,0:T(8,128)(2,1)S(1)}, u32[]{:S(2)}, u32[]{:S(2)}) collective-permute-start(bf16[40,7168]{1,0:T(8,128)(2,1)} %weights.1), channel_id=1, source_target_pairs={{0,1},{1,0},{2,3},{3,2},{4,5},{5,4},{6,7},{7,6},{8,9},{9,8},{10,11... | collective-permute-start | bytes 1720328 | tf_op jit(solution)/shard_map/ppermute | solution.py:57
  21.2 0.0 copy-start.3
  21.2 0.7 copy-done.3
  21.8 0.0 copy-start.4
  21.8 0.0 copy-start.5
  21.8 0.0 copy-start.7
  21.9 0.0 copy-start
  21.9 3.3 %pick.1 = bf16[64,8,128]{2,1,0:T(8,128)(2,1)} custom-call(s32[1]{0:T(128)} %bitcast.6.rank, s32[2,4]{1,0:T(2,128)S(1)} %bitcast.19, bf16[594,5120]{1,0:T(8,128)(2,1)} %refs_7_.1, bf16[594,5120]{1,0:T(8,128)(2,1)} %refs_7_.1, bf16[594,5120]{1,0:T(8,128)(2,1)} %refs_7_.1, bf16[594,5120]{1,0:T(8,128)(2,1)} %refs_7_.1, bf16[594,5120]{1,0:T(8,128)(2,1)} %refs_7_.1, ...), custom_call_target="tpu_custom_call" | custom-call | tf_op jit(solution)/shard_map/pick/pallas_call | solution.py:109
  25.1 0.0 copy-start.2
  25.1 6.6 %all-to-all-start = ((bf16[64,8,128]{2,1,0:T(8,128)(2,1)}), bf16[64,8,128]{2,1,0:T(8,128)(2,1)S(1)}, u32[]{:S(2)}, u32[]{:S(2)}) async-start(bf16[64,8,128]{2,1,0:T(8,128)(2,1)} %pick.1), calls=%async_computation | async-start | bytes 262144 | tf_op jit(solution)/shard_map/all_to_all | solution.py:53
  31.7 0.0 copy-done.4
  31.7 0.2 collective-permute-start.2
  31.9 0.0 copy-done.5
  31.9 0.5 collective-permute-start.3
  32.4 0.0 copy-done.7
  32.4 9.6 %all-to-all-done = bf16[64,8,128]{2,1,0:T(8,128)(2,1)S(1)} async-done(((bf16[64,8,128]{2,1,0:T(8,128)(2,1)}), bf16[64,8,128]{2,1,0:T(8,128)(2,1)S(1)}, u32[]{:S(2)}, u32[]{:S(2)}) %all-to-all-start) | async-done | bytes 131104 | tf_op jit(solution)/shard_map/all_to_all | solution.py:53
  42.0 0.1 convert_reduce_fusion.1.own
  42.1 2.2 %collective-permute-start = (f32[8,128]{1,0:T(8,128)S(1)}, f32[8,128]{1,0:T(8,128)S(1)}, u32[]{:S(2)}, u32[]{:S(2)}) collective-permute-start(f32[8,128]{1,0:T(8,128)S(1)} %convert_reduce_fusion.1.own), channel_id=1, source_target_pairs={{0,1},{1,0},{2,3},{3,2},{4,5},{5,4},{6,7},{7,6},{8,9},{9,8},{10,11... | collective-permute-start | bytes 12296 | tf_op jit(solution)/shard_map/ppermute | solution.py:57
  44.3 0.8 bitcast_convert_fusion.gain
  45.0 0.1 convert_element_type.25
  45.1 0.0 collective-permute-done.other
  45.1 0.0 collective-permute-done.1.other_weights
  45.1 0.0 copy-done
  45.1 1.4 joint.1
  46.5 6.5 %all-to-all-start.1 = ((bf16[64,8,128]{2,1,0:T(8,128)(2,1)}), bf16[64,8,128]{2,1,0:T(8,128)(2,1)S(1)}, u32[]{:S(2)}, u32[]{:S(2)}) async-start(bf16[64,8,128]{2,1,0:T(8,128)(2,1)} %get-tuple-element.7), calls=%async_computation.1 | async-start | bytes 262144 | tf_op jit(solution)/shard_map/all_to_all | solution.py:53
  53.0 0.1 fusion
  53.1 0.1 pad_add_fusion.place
  53.2 0.1 pad_maximum_fusion
  53.3 10.0 %all-to-all-done.1.got = bf16[64,8,128]{2,1,0:T(8,128)(2,1)S(1)} async-done(((bf16[64,8,128]{2,1,0:T(8,128)(2,1)}), bf16[64,8,128]{2,1,0:T(8,128)(2,1)S(1)}, u32[]{:S(2)}, u32[]{:S(2)}) %all-to-all-start.1) | async-done | bytes 131104 | tf_op jit(solution)/shard_map/all_to_all | solution.py:53
  63.3 0.0 copy-done.2
  63.3 1.3 rotate.1
  64.6 6.5 %all-to-all-start.2 = ((bf16[64,8,128]{2,1,0:T(8,128)(2,1)}), bf16[64,8,128]{2,1,0:T(8,128)(2,1)S(1)}, u32[]{:S(2)}, u32[]{:S(2)}) async-start(bf16[64,8,128]{2,1,0:T(8,128)(2,1)} %rotate.1), calls=%async_computation.2 | async-start | bytes 262144 | tf_op jit(solution)/shard_map/all_to_all | solution.py:53
  71.1 0.1 stack.32.info
  71.2 0.0 copy-start.1
  71.2 0.0 collective-permute-done.2.other_keys
  71.2 0.0 collective-permute-done.3.other_values
  71.2 10.1 %all-to-all-done.2.heads = bf16[64,8,128]{2,1,0:T(8,128)(2,1)S(1)} async-done(((bf16[64,8,128]{2,1,0:T(8,128)(2,1)}), bf16[64,8,128]{2,1,0:T(8,128)(2,1)S(1)}, u32[]{:S(2)}, u32[]{:S(2)}) %all-to-all-start.2) | async-done | bytes 131104 | tf_op jit(solution)/shard_map/all_to_all | solution.py:53
  81.3 4.2 %attend.1 = bf16[64,8,128]{2,1,0:T(8,128)(2,1)} custom-call(s32[6]{0:T(128)S(1)} %stack.32.info, bf16[64,8,128]{2,1,0:T(8,128)(2,1)S(1)} %all-to-all-done.2.heads, bf16[2,256,1024]{2,1,0:T(8,128)(2,1)} %keys.1, bf16[2,256,1024]{2,1,0:T(8,128)(2,1)} %collective-permute-done.2.other_keys, bf16[2,256,1024]{2,1,0:T(8,128)(2,1)} %values.1, ...), custom_call_target="tpu_custom_call" | custom-call | tf_op jit(solution)/shard_map/attend/pallas_call | solution.py:232
  85.5 0.0 copy-start.6
  85.6 6.6 %all-to-all-start.3 = ((bf16[64,8,128]{2,1,0:T(8,128)(2,1)}), bf16[64,8,128]{2,1,0:T(8,128)(2,1)S(1)}, u32[]{:S(2)}, u32[]{:S(2)}) async-start(bf16[64,8,128]{2,1,0:T(8,128)(2,1)} %attend.1), calls=%async_computation.3 | async-start | bytes 262144 | tf_op jit(solution)/shard_map/all_to_all | solution.py:53
  92.2 0.0 copy-done.1
  92.2 3.5 %collective-permute-start.5 = (bf16[40,5120]{1,0:T(8,128)(2,1)S(1)}, bf16[40,5120]{1,0:T(8,128)(2,1)S(1)}, u32[]{:S(2)}, u32[]{:S(2)}) collective-permute-start(bf16[40,5120]{1,0:T(8,128)(2,1)S(1)} %bitcast.15), channel_id=1, source_target_pairs={{0,1},{1,0},{2,3},{3,2},{4,5},{5,4},{6,7},{7,6},{8,9},{9,8},{10,11... | collective-permute-start | bytes 1228808 | tf_op jit(solution)/shard_map/ppermute | solution.py:57
  95.7 6.7 %all-to-all-done.3.got = bf16[64,8,128]{2,1,0:T(8,128)(2,1)S(1)} async-done(((bf16[64,8,128]{2,1,0:T(8,128)(2,1)}), bf16[64,8,128]{2,1,0:T(8,128)(2,1)S(1)}, u32[]{:S(2)}, u32[]{:S(2)}) %all-to-all-start.3) | async-done | bytes 131104 | tf_op jit(solution)/shard_map/all_to_all | solution.py:53
  102.4 0.4 merge.1
  102.9 16.8 %all_to_all.35.own = bf16[64,8,128]{2,1,0:T(8,128)(2,1)S(1)} all-to-all(bf16[64,8,128]{2,1,0:T(8,128)(2,1)S(1)} %merge.1), channel_id=1, replica_groups=mesh['parts'=2,'seq_0'=8,'seq_1'=8,'seq_2'=2] {'seq_0','seq_1'}, dimensions={0} | all-to-all | bytes 262144 | tf_op jit(solution)/shard_map/all_to_all | solution.py:53
  119.6 4.7 %collective-permute-start.4 = (bf16[64,8,128]{2,1,0:T(8,128)(2,1)S(1)}, bf16[64,8,128]{2,1,0:T(8,128)(2,1)S(1)}, u32[]{:S(2)}, u32[]{:S(2)}) collective-permute-start(bf16[64,8,128]{2,1,0:T(8,128)(2,1)S(1)} %all_to_all.35.own), channel_id=1, source_target_pairs={{0,1},{1,0},{2,3},{3,2},{4,5},{5,4},{6,7},{7,6},{8,9},{9,8},{10,11... | collective-permute-start | bytes 393224 | tf_op jit(solution)/shard_map/ppermute | solution.py:57
  124.3 0.0 collective-permute-done.5.other_weights
  124.3 1.0 collective-permute-done.4.other
  125.3 1.6 project.1
  126.9 6.5 %all-to-all-start.5 = ((bf16[64,8,128]{2,1,0:T(8,128)(2,1)}), bf16[64,8,128]{2,1,0:T(8,128)(2,1)S(1)}, u32[]{:S(2)}, u32[]{:S(2)}) async-start(bf16[64,8,128]{2,1,0:T(8,128)(2,1)} %get-tuple-element.11), calls=%async_computation.5 | async-start | bytes 262144 | tf_op jit(solution)/shard_map/all_to_all | solution.py:53
  133.4 0.0 copy-done.6
  133.4 10.2 %all-to-all-done.5.got = bf16[64,8,128]{2,1,0:T(8,128)(2,1)S(1)} async-done(((bf16[64,8,128]{2,1,0:T(8,128)(2,1)}), bf16[64,8,128]{2,1,0:T(8,128)(2,1)S(1)}, u32[]{:S(2)}, u32[]{:S(2)}) %all-to-all-start.5) | async-done | bytes 131104 | tf_op jit(solution)/shard_map/all_to_all | solution.py:53
  143.6 2.5 %mlp.1 = bf16[64,8,128]{2,1,0:T(8,128)(2,1)S(1)} custom-call(bf16[64,8,128]{2,1,0:T(8,128)(2,1)S(1)} %all-to-all-done.5.got, f32[1,5120]{1,0:T(1,128)S(1)} %bitcast.17, bf16[5120,128]{1,0:T(8,128)(2,1)} %w_gate.1, bf16[5120,128]{1,0:T(8,128)(2,1)} %w_up.1, bf16[128,5120]{1,0:T(8,128)(2,1)} %w_down.1), custom_call_target="tpu_custom_call" | custom-call | tf_op jit(solution)/shard_map/mlp/pallas_call | solution.py:413
  146.2 16.0 %all_to_all.36 = bf16[64,8,128]{2,1,0:T(8,128)(2,1)S(1)} all-to-all(bf16[64,8,128]{2,1,0:T(8,128)(2,1)S(1)} %mlp.1), channel_id=1, replica_groups=mesh['parts'=2,'seq_0'=8,'seq_1'=8,'seq_2'=2] {'seq_0','seq_1'}, dimensions={0} | all-to-all | bytes 262144 | tf_op jit(solution)/shard_map/all_to_all | solution.py:53
  162.2 0.1 convert_reduce_fusion
  162.3 3.3 %collective-permute-start.6 = (f32[8,128]{1,0:T(8,128)S(1)}, f32[8,128]{1,0:T(8,128)S(1)}, u32[]{:S(2)}, u32[]{:S(2)}) collective-permute-start(f32[8,128]{1,0:T(8,128)S(1)} %convert_reduce_fusion), channel_id=1, source_target_pairs={{0,1},{1,0},{2,3},{3,2},{4,5},{5,4},{6,7},{7,6},{8,9},{9,8},{10,11... | collective-permute-start | bytes 12296 | tf_op jit(solution)/shard_map/ppermute | solution.py:57
  165.5 0.7 reshape.43
  166.2 0.2 collective-permute-done.6
  166.4 0.7 select_convert_fusion
  (5 shorter events, 0.0 us)
Async XLA Ops:
  0.6 44.5 %collective-permute-start.1 = (bf16[40,7168]{1,0:T(8,128)(2,1)}, bf16[40,7168]{1,0:T(8,128)(2,1)S(1)}, u32[]{:S(2)}, u32[]{:S(2)}) collective-permute-start(bf16[40,7168]{1,0:T(8,128)(2,1)} %weights.1), channel_id=1, source_target_pairs={{0,1},{1,0},{2,3},{3,2},{4,5},{5,4},{6,7},{7,6},{8,9},{9,8},{10,11... | collective-permute-start | bytes 1720328 | tf_op jit(solution)/shard_map/ppermute | solution.py:57
  21.2 0.7 copy-start.3
  21.8 9.9 %copy-start.4 = (bf16[2,256,1024]{2,1,0:T(8,128)(2,1)S(1)}, bf16[2,256,1024]{2,1,0:T(8,128)(2,1)}, u32[]{:S(2)}) copy-start(bf16[2,256,1024]{2,1,0:T(8,128)(2,1)} %keys.1) | copy-start | bytes 3145732
  21.8 10.0 %copy-start.5 = (bf16[2,256,1024]{2,1,0:T(8,128)(2,1)S(1)}, bf16[2,256,1024]{2,1,0:T(8,128)(2,1)}, u32[]{:S(2)}) copy-start(bf16[2,256,1024]{2,1,0:T(8,128)(2,1)} %values.1) | copy-start | bytes 3145732
  21.8 10.5 %copy-start.7 = (s32[2]{0:T(128)S(1)}, s32[2]{0:T(128)}, u32[]{:S(2)}) copy-start(s32[2]{0:T(128)} %param.14) | copy-start | bytes 28
  21.9 23.3 %copy-start = (bf16[40,7168]{1,0:T(8,128)(2,1)S(1)}, bf16[40,7168]{1,0:T(8,128)(2,1)}, u32[]{:S(2)}) copy-start(bf16[40,7168]{1,0:T(8,128)(2,1)} %weights.1) | copy-start | bytes 1720324
  25.1 38.1 %copy-start.2 = (f32[7168]{0:T(1024)S(1)}, f32[7168]{0:T(1024)}, u32[]{:S(2)}) copy-start(f32[7168]{0:T(1024)} %param.18) | copy-start | bytes 86020
  25.1 16.9 %all-to-all-start = ((bf16[64,8,128]{2,1,0:T(8,128)(2,1)}), bf16[64,8,128]{2,1,0:T(8,128)(2,1)S(1)}, u32[]{:S(2)}, u32[]{:S(2)}) async-start(bf16[64,8,128]{2,1,0:T(8,128)(2,1)} %pick.1), calls=%async_computation | async-start | bytes 262144 | tf_op jit(solution)/shard_map/all_to_all | solution.py:53
  31.7 39.4 %collective-permute-start.2 = (bf16[2,256,1024]{2,1,0:T(8,128)(2,1)S(1)}, bf16[2,256,1024]{2,1,0:T(8,128)(2,1)}, u32[]{:S(2)}, u32[]{:S(2)}) collective-permute-start(bf16[2,256,1024]{2,1,0:T(8,128)(2,1)S(1)} %copy-done.4), channel_id=1, source_target_pairs={{0,1},{1,0},{2,3},{3,2},{4,5},{5,4},{6,7},{7,6},{8,9},{9,8},{10,11... | collective-permute-start | bytes 3145736 | tf_op jit(solution)/shard_map/ppermute | solution.py:57
  31.9 39.3 %collective-permute-start.3 = (bf16[2,256,1024]{2,1,0:T(8,128)(2,1)S(1)}, bf16[2,256,1024]{2,1,0:T(8,128)(2,1)}, u32[]{:S(2)}, u32[]{:S(2)}) collective-permute-start(bf16[2,256,1024]{2,1,0:T(8,128)(2,1)S(1)} %copy-done.5), channel_id=1, source_target_pairs={{0,1},{1,0},{2,3},{3,2},{4,5},{5,4},{6,7},{7,6},{8,9},{9,8},{10,11... | collective-permute-start | bytes 3145736 | tf_op jit(solution)/shard_map/ppermute | solution.py:57
  42.1 3.0 %collective-permute-start = (f32[8,128]{1,0:T(8,128)S(1)}, f32[8,128]{1,0:T(8,128)S(1)}, u32[]{:S(2)}, u32[]{:S(2)}) collective-permute-start(f32[8,128]{1,0:T(8,128)S(1)} %convert_reduce_fusion.1.own), channel_id=1, source_target_pairs={{0,1},{1,0},{2,3},{3,2},{4,5},{5,4},{6,7},{7,6},{8,9},{9,8},{10,11... | collective-permute-start | bytes 12296 | tf_op jit(solution)/shard_map/ppermute | solution.py:57
  46.5 16.8 %all-to-all-start.1 = ((bf16[64,8,128]{2,1,0:T(8,128)(2,1)}), bf16[64,8,128]{2,1,0:T(8,128)(2,1)S(1)}, u32[]{:S(2)}, u32[]{:S(2)}) async-start(bf16[64,8,128]{2,1,0:T(8,128)(2,1)} %get-tuple-element.7), calls=%async_computation.1 | async-start | bytes 262144 | tf_op jit(solution)/shard_map/all_to_all | solution.py:53
  64.6 16.7 %all-to-all-start.2 = ((bf16[64,8,128]{2,1,0:T(8,128)(2,1)}), bf16[64,8,128]{2,1,0:T(8,128)(2,1)S(1)}, u32[]{:S(2)}, u32[]{:S(2)}) async-start(bf16[64,8,128]{2,1,0:T(8,128)(2,1)} %rotate.1), calls=%async_computation.2 | async-start | bytes 262144 | tf_op jit(solution)/shard_map/all_to_all | solution.py:53
  71.2 21.0 %copy-start.1 = (bf16[5120,40]{0,1:T(8,128)(2,1)S(1)}, bf16[5120,40]{0,1:T(8,128)(2,1)}, u32[]{:S(2)}) copy-start(bf16[5120,40]{0,1:T(8,128)(2,1)} %param.21) | copy-start | bytes 1228804
  85.5 47.9 %copy-start.6 = (bf16[5120]{0:T(1024)(128)(2,1)S(1)}, bf16[5120]{0:T(1024)(128)(2,1)}, u32[]{:S(2)}) copy-start(bf16[5120]{0:T(1024)(128)(2,1)} %param.22) | copy-start | bytes 30724
  85.6 16.9 %all-to-all-start.3 = ((bf16[64,8,128]{2,1,0:T(8,128)(2,1)}), bf16[64,8,128]{2,1,0:T(8,128)(2,1)S(1)}, u32[]{:S(2)}, u32[]{:S(2)}) async-start(bf16[64,8,128]{2,1,0:T(8,128)(2,1)} %attend.1), calls=%async_computation.3 | async-start | bytes 262144 | tf_op jit(solution)/shard_map/all_to_all | solution.py:53
  92.2 32.2 %collective-permute-start.5 = (bf16[40,5120]{1,0:T(8,128)(2,1)S(1)}, bf16[40,5120]{1,0:T(8,128)(2,1)S(1)}, u32[]{:S(2)}, u32[]{:S(2)}) collective-permute-start(bf16[40,5120]{1,0:T(8,128)(2,1)S(1)} %bitcast.15), channel_id=1, source_target_pairs={{0,1},{1,0},{2,3},{3,2},{4,5},{5,4},{6,7},{7,6},{8,9},{9,8},{10,11... | collective-permute-start | bytes 1228808 | tf_op jit(solution)/shard_map/ppermute | solution.py:57
  119.6 5.7 %collective-permute-start.4 = (bf16[64,8,128]{2,1,0:T(8,128)(2,1)S(1)}, bf16[64,8,128]{2,1,0:T(8,128)(2,1)S(1)}, u32[]{:S(2)}, u32[]{:S(2)}) collective-permute-start(bf16[64,8,128]{2,1,0:T(8,128)(2,1)S(1)} %all_to_all.35.own), channel_id=1, source_target_pairs={{0,1},{1,0},{2,3},{3,2},{4,5},{5,4},{6,7},{7,6},{8,9},{9,8},{10,11... | collective-permute-start | bytes 393224 | tf_op jit(solution)/shard_map/ppermute | solution.py:57
  126.9 16.7 %all-to-all-start.5 = ((bf16[64,8,128]{2,1,0:T(8,128)(2,1)}), bf16[64,8,128]{2,1,0:T(8,128)(2,1)S(1)}, u32[]{:S(2)}, u32[]{:S(2)}) async-start(bf16[64,8,128]{2,1,0:T(8,128)(2,1)} %get-tuple-element.11), calls=%async_computation.5 | async-start | bytes 262144 | tf_op jit(solution)/shard_map/all_to_all | solution.py:53
  162.3 4.1 %collective-permute-start.6 = (f32[8,128]{1,0:T(8,128)S(1)}, f32[8,128]{1,0:T(8,128)S(1)}, u32[]{:S(2)}, u32[]{:S(2)}) collective-permute-start(f32[8,128]{1,0:T(8,128)S(1)} %convert_reduce_fusion), channel_id=1, source_target_pairs={{0,1},{1,0},{2,3},{3,2},{4,5},{5,4},{6,7},{7,6},{8,9},{9,8},{10,11... | collective-permute-start | bytes 12296 | tf_op jit(solution)/shard_map/ppermute | solution.py:57

commit v2 on v1

--- a/solution.py
+++ b/solution.py
@@ -168,9 +168,22 @@
     out[...] = jnp.broadcast_to(result[None], out.shape)
 
 
-def attend_kernel(info, heads, keys, other_keys, values, other_values, out):
+def attend_kernel(
+    info, heads, keys, other_keys, values, other_values, out, key_parts, value_parts, sems
+):
     tokens = heads.shape[1]
-    batch, local_len, _ = keys.shape
+    _, batch, local_len, cut = key_parts.shape
+    columns = pl.ds(pl.multiple_of(info[0] * cut, cut), cut)
+    copies = []
+    for n, (mine, others, parts) in enumerate(
+        ((keys, other_keys, key_parts), (values, other_values, value_parts))
+    ):
+        for side, source in enumerate((mine, others)):
+            copy = pltpu.make_async_copy(
+                source.at[:, :, columns], parts.at[side], sems.at[n, side]
+            )
+            copy.start()
+            copies.append(copy)
     rows = GROUP * tokens
     score_scale = 1.0 / math.sqrt(HEAD_DIM)
     token = lax.broadcasted_iota(jnp.int32, (rows, 1), 0) % tokens
@@ -178,69 +191,82 @@
     spot = lax.broadcasted_iota(jnp.int32, (1, local_len), 1)
     fresh = lax.broadcasted_iota(jnp.int32, (1, tokens), 1)
     fresh_valid = (fresh % batch == prompt) & (fresh <= token) & (info[3] > 0)
+    fresh_mask = jnp.where(fresh_valid, 0.0, MASKED)
+    chunks = [(side, b) for side in range(2) for b in range(batch)]
+    mask = jnp.concatenate(
+        [
+            jnp.where((spot + info[1 + side] < info[4 + b]) & (prompt == b), 0.0, MASKED)
+            for side, b in chunks
+        ],
+        axis=1,
+    )
     contract = (((1,), (1,)), ((), ()))
     lane = lanes((tokens, HEAD_DIM))
-    valid = [
-        [(spot + info[1 + side] < info[4 + b]) & (prompt == b) for b in range(batch)]
-        for side in range(2)
+    used = 2 * Q_HALF
+    out[used:] = jnp.zeros((out.shape[0] - used, *out.shape[1:]), BF16)
+    places = [slice(h * HEAD_DIM, (h + 1) * HEAD_DIM) for h in range(KV_HALF)]
+    queries = [
+        heads[h * GROUP : (h + 1) * GROUP].astype(F32).reshape(rows, HEAD_DIM).astype(BF16)
+        for h in range(KV_HALF)
     ]
+    fresh_scores = [
+        lax.dot_general(queries[h], heads[Q_HALF + h], contract, preferred_element_type=F32)
+        * score_scale
+        + fresh_mask
+        for h in range(KV_HALF)
+    ]
+    copies[0].wait()
+    copies[1].wait()
+    scores = []
     for h in range(KV_HALF):
-        columns = slice(h * HEAD_DIM, (h + 1) * HEAD_DIM)
-        query = heads[h * GROUP : (h + 1) * GROUP].astype(F32).reshape(rows, HEAD_DIM).astype(BF16)
-        scores, kept, matching = [], [], []
-        for side, (k_ref, v_ref) in enumerate(((keys, values), (other_keys, other_values))):
-            for b in range(batch):
-                score = lax.dot_general(
-                    query, k_ref[b, :, columns], contract, preferred_element_type=F32
-                )
-                scores.append(jnp.where(valid[side][b], score * score_scale, MASKED))
-                kept.append(valid[side][b])
-                matching.append(v_ref[b, :, columns])
-        score = lax.dot_general(
-            query, heads[Q_HALF + h], contract, preferred_element_type=F32
+        found = [
+            lax.dot_general(
+                queries[h], key_parts[side, b, :, places[h]], contract, preferred_element_type=F32
+            )
+            for side, b in chunks
+        ]
+        scores.append(jnp.concatenate(found, axis=1) * score_scale + mask)
+    tops = [
+        jnp.maximum(
+            jnp.maximum(
+                jnp.max(scores[h], axis=-1, keepdims=True),
+                jnp.max(fresh_scores[h], axis=-1, keepdims=True),
+            ),
+            0.1 * MASKED,
         )
-        scores.append(jnp.where(fresh_valid, score * score_scale, MASKED))
-        kept.append(fresh_valid)
-        matching.append(heads[Q_HALF + KV_HALF + h])
-        top = functools.reduce(
-            jnp.maximum, [jnp.max(s, axis=-1, keepdims=True) for s in scores]
+        for h in range(KV_HALF)
+    ]
+    weights = [jnp.exp(scores[h] - tops[h]) for h in range(KV_HALF)]
+    fresh_weights = [jnp.exp(fresh_scores[h] - tops[h]) for h in range(KV_HALF)]
+    totals = [
+        jnp.sum(weights[h], axis=-1, keepdims=True)
+        + jnp.sum(fresh_weights[h], axis=-1, keepdims=True)
+        for h in range(KV_HALF)
+    ]
+    weights = [weight.astype(BF16) for weight in weights]
+    copies[2].wait()
+    copies[3].wait()
+    for h in range(KV_HALF):
+        summed = jnp.dot(
+            fresh_weights[h].astype(BF16),
+            heads[Q_HALF + KV_HALF + h],
+            preferred_element_type=F32,
         )
-        total = jnp.zeros((rows, 1), F32)
-        summed = jnp.zeros((rows, HEAD_DIM), F32)
-        for s, keep, value in zip(scores, kept, matching):
-            weight = jnp.where(keep, jnp.exp(s - top), 0.0)
-            total += jnp.sum(weight, axis=-1, keepdims=True)
-            summed += jnp.dot(weight.astype(BF16), value, preferred_element_type=F32)
+        for n, (side, b) in enumerate(chunks):
+            summed += jnp.dot(
+                weights[h][:, n * local_len : (n + 1) * local_len],
+                value_parts[side, b, :, places[h]],
+                preferred_element_type=F32,
+            )
         for g in range(GROUP):
             part = slice(g * tokens, (g + 1) * tokens)
             extra = jnp.zeros(lane.shape, F32)
-            for i, piece in enumerate(in_pieces(top[part]) + in_pieces(total[part])):
+            for i, piece in enumerate(in_pieces(tops[h][part]) + in_pieces(totals[h][part])):
                 extra = jnp.where(lane == HALF + i, piece, extra)
             both = summed[part]
             at = 2 * (h * GROUP + g)
             out[at] = jnp.where(lane < HALF, both, extra).astype(BF16)
             out[at + 1] = jnp.where(lane < HALF, pltpu.roll(both, HALF, 1), extra).astype(BF16)
-    used = 2 * Q_HALF
-    out[used:] = jnp.zeros((out.shape[0] - used, *out.shape[1:]), BF16)
-
-
-def attend(info, heads, keys, other_keys, values, other_values):
-    batch, local_len, key_width = keys.shape
-    cut = key_width // 2
-    whole = pl.BlockSpec(heads.shape, lambda _, i: (0, 0, 0))
-    mine = pl.BlockSpec((batch, local_len, cut), lambda _, i: (0, 0, i[0]))
-    return pl.pallas_call(
-        attend_kernel,
-        out_shape=jax.ShapeDtypeStruct(heads.shape, BF16),
-        grid_spec=pltpu.PrefetchScalarGridSpec(
-            num_scalar_prefetch=1,
-            grid=(1,),
-            in_specs=[whole, mine, mine, mine, mine],
-            out_specs=whole,
-        ),
-        compiler_params=grant(53),
-        name="attend",
-    )(info, heads, keys, other_keys, values, other_values)
 
 
 def merge_kernel(got, out):
@@ -254,7 +280,19 @@
 
 
 def project_kernel(
-    core, own, other, weights, other_weights, stream, attended, mid_out, out, held, other_held, sems
+    core,
+    own,
+    other,
+    weights,
+    other_weights,
+    stream,
+    attended,
+    mid_out,
+    out,
+    rows_held,
+    held,
+    other_held,
+    sems,
 ):
     copies = [
         pltpu.make_async_copy(weights, held, sems.at[0]),
@@ -270,8 +308,12 @@
             low = pieces[2 * i].astype(F32)
             high = pltpu.roll(pieces[2 * i + 1].astype(F32), HALF, 1)
             column = pl.multiple_of((start + i) * HEAD_DIM, HEAD_DIM)
-            attended[:, pl.ds(column, HEAD_DIM)] = jnp.where(lane < HALF, low, high).astype(BF16)
-    rows = attended[...]
+            both = jnp.where(lane < HALF, low, high).astype(BF16)
+            rows_held[:, pl.ds(column, HEAD_DIM)] = both
+    rows = rows_held[...]
+    steps, batch, _ = attended.shape
+    for step in range(steps):
+        attended[step] = rows[step * batch : (step + 1) * batch]
     contract = (((1,), (1,)), ((), ()))
     for copy in copies:
         copy.wait()
@@ -346,17 +388,6 @@
     own_out = w_out.T
     other_out = partner(own_out)
 
-    sent = pick(rank.reshape(1), token_ids.T, embed_table, chips)
-    got = jnp.sum(swap(sent).astype(F32), axis=0)
-    gain = lax.dynamic_slice_in_dim(attn_gain, j * width, width, 0).astype(F32)[None]
-    sent, stream = kernel_call(
-        joint_kernel,
-        (jax.ShapeDtypeStruct(tile, BF16), jax.ShapeDtypeStruct((tokens, width), F32)),
-        [SCALARS] + [WHOLE] * 3 + [STAYS] * 2,
-        [pltpu.VMEM((features, BLOCKS * HEAD_DIM), BF16)] * 2 + [pltpu.SemaphoreType.DMA((3, 2))],
-        name="joint",
-    )(core, got, partner(got), gain, w_qkv, other_qkv)
-
     positions = (lengths[None, :] + jnp.arange(steps, dtype=jnp.int32)[:, None]).reshape(-1)
     frequency = ROPE_BASE ** (-2.0 * jnp.arange(HALF, dtype=F32) / HEAD_DIM)
     angles = positions.astype(F32)[:, None] * frequency
@@ -375,14 +406,6 @@
     )
     head = jnp.where(j < BLOCKS, head, 0)
     place = jnp.stack([head, (j < Q_HALF + KV_HALF).astype(jnp.int32)])
-    heads = kernel_call(
-        rotate_kernel,
-        jax.ShapeDtypeStruct(tile, BF16),
-        [SCALARS] + [WHOLE] * 4,
-        name="rotate",
-    )(place, swap(sent), qkv_bias.reshape(-1, HEAD_DIM), cosine, sine)
-    heads = swap(heads)
-
     info = jnp.stack(
         [
             c,
@@ -392,7 +415,51 @@
             *[lengths[b] for b in range(batch)],
         ]
     )
-    partial = attend(info, heads, cache_keys, other_keys, cache_values, other_values)
+    sent = pick(rank.reshape(1), token_ids.T, embed_table, chips)
+    got = jnp.sum(swap(sent).astype(F32), axis=0)
+    gain = lax.dynamic_slice_in_dim(attn_gain, j * width, width, 0).astype(F32)[None]
+    sent, stream = kernel_call(
+        joint_kernel,
+        (jax.ShapeDtypeStruct(tile, BF16), jax.ShapeDtypeStruct((tokens, width), F32)),
+        [SCALARS] + [WHOLE] * 3 + [STAYS] * 2,
+        [pltpu.VMEM((features, BLOCKS * HEAD_DIM), BF16)] * 2 + [pltpu.SemaphoreType.DMA((3, 2))],
+        name="joint",
+    )(core, got, partner(got), gain, w_qkv, other_qkv)
+
+    sent, place, cosine, sine, info, bias, mlp_gain, other_keys, other_values, other_out = (
+        lax.optimization_barrier(
+            (
+                sent,
+                place,
+                cosine,
+                sine,
+                info,
+                qkv_bias.reshape(-1, HEAD_DIM),
+                mlp_gain.astype(F32)[None],
+                other_keys,
+                other_values,
+                other_out,
+            )
+        )
+    )
+
+    heads = kernel_call(
+        rotate_kernel,
+        jax.ShapeDtypeStruct(tile, BF16),
+        [SCALARS] + [WHOLE] * 4,
+        name="rotate",
+    )(place, swap(sent), bias, cosine, sine)
+    heads = swap(heads)
+
+    parts = (2, batch, local_len, KV_HALF * HEAD_DIM)
+    partial = kernel_call(
+        attend_kernel,
+        jax.ShapeDtypeStruct(tile, BF16),
+        [SCALARS, WHOLE] + [STAYS] * 4,
+        [pltpu.VMEM(parts, BF16)] * 2 + [pltpu.SemaphoreType.DMA((2, 2))],
+        name="attend",
+        room=53,
+    )(info, heads, cache_keys, other_keys, cache_values, other_values)
     merged = kernel_call(merge_kernel, jax.ShapeDtypeStruct(tile, BF16), [WHOLE], name="merge")(
         swap(partial)
     )
@@ -401,12 +468,14 @@
     attended, mid, sent = kernel_call(
         project_kernel,
         (
-            jax.ShapeDtypeStruct((tokens, HEADS * HEAD_DIM), BF16),
+            jax.ShapeDtypeStruct((steps, batch, HEADS * HEAD_DIM), BF16),
             jax.ShapeDtypeStruct((tokens, width), F32),
             jax.ShapeDtypeStruct(tile, BF16),
         ),
         [SCALARS] + [WHOLE] * 2 + [STAYS] * 2 + [WHOLE],
-        [pltpu.VMEM(own_out.shape, BF16)] * 2 + [pltpu.SemaphoreType.DMA((2,))],
+        [pltpu.VMEM((tokens, HEADS * HEAD_DIM), BF16)]
+        + [pltpu.VMEM(own_out.shape, BF16)] * 2
+        + [pltpu.SemaphoreType.DMA((2,))],
         name="project",
     )(core, pieces, partner(pieces), own_out, other_out, stream)
 
@@ -421,12 +490,12 @@
         ],
         name="mlp",
         room=53,
-    )(swap(sent), mlp_gain.astype(F32)[None], w_gate, w_up, w_down)
+    )(swap(sent), mlp_gain, w_gate, w_up, w_down)
     summed = jnp.sum(swap(down).astype(F32), axis=0)
     summed = mid + (summed + partner(summed))[:, :width]
     mine = jnp.where(c == 0, summed[:, :features], summed[:, features:])
     layer_out = mine.astype(BF16).reshape(steps, batch, features)
-    return (attended.reshape(steps, batch, -1), layer_out)
+    return (attended, layer_out)
 
 
 def solution(mesh):

time: 168 us -> 161 us (0.958)
  blocking collectives: 32.8 us -> 95.8 us
  waiting for transfers between devices: 47.8 us -> 11 us
  starting transfers between devices: 67.4 us -> 38.8 us
  Pallas kernels: 14.8 us -> 11.5 us
    all_to_all x2 -> x6, blocking collectives: 32.8 us -> 95.8 us  [swap(): return lax.all_to_all(parts, CHIPS, 0, 0)]
    all_to_all x5 -> x1, waiting for transfers between devices: 46.7 us -> 9.17 us  [swap(): return lax.all_to_all(parts, CHIPS, 0, 0)]
    all_to_all x5 -> x1, starting transfers between devices: 32.6 us -> 6.61 us  [swap(): return lax.all_to_all(parts, CHIPS, 0, 0)]
    ppermute x7, starting transfers between devices: 34.8 us -> 32.2 us  [partner(): return lax.ppermute(array, CORE, [(0, 1), (1, 0)])]
    pallas_call x2, Pallas kernels: 5.85 us -> 4.01 us  [the longest x1 2.83 us: body(): kernel_call(attend_kernel, jax.ShapeDtypeStruct(tile, BF16), [SCALARS, WH...]
  transfers between devices with their start and end apart: 12 -> 8, of which waited for: 7 -> 3; matrix products, arithmetic and copies ran while one was open for 1% -> 1% of each run, Pallas kernels for 4% -> 2%
where the time goes in v2:
time: 161 us
  blocking collectives  95.8 us (60%)
  starting transfers between devices  38.8 us (24%)
  Pallas kernels  11.5 us (7%)
  waiting for transfers between devices  11 us (7%)
  other arithmetic  1.84 us (1%)
    all_to_all x6, blocking collectives, swap(): return lax.all_to_all(parts, CHIPS, 0, 0)  95.8 us
    ppermute x7, starting transfers between devices, partner(): return lax.ppermute(array, CORE, [(0, 1), (1, 0)])  32.2 us
    all_to_all x1, waiting for transfers between devices, swap(): return lax.all_to_all(parts, CHIPS, 0, 0)  9.17 us
    all_to_all x1, starting transfers between devices, swap(): return lax.all_to_all(parts, CHIPS, 0, 0)  6.61 us
  transfers between devices with their start and end apart: 8, of which 3 were waited for; matrix products, arithmetic and copies ran while one was open for 1% of the time, Pallas kernels for 2%

profile of v2, /device:TPU:513, one launch (start us, length us, event | category | flops | bytes accessed | tf_op | source)
XLA Modules:
  0.0 160.6 jit_solution(8276657835433279884)
XLA Ops:
  0.6 20.5 %collective-permute-start.2 = (bf16[2,256,1024]{2,1,0:T(8,128)(2,1)}, bf16[2,256,1024]{2,1,0:T(8,128)(2,1)S(1)}, u32[]{:S(2)}, u32[]{:S(2)}) collective-permute-start(bf16[2,256,1024]{2,1,0:T(8,128)(2,1)} %keys.1), channel_id=1, source_target_pairs={{0,1},{1,0},{2,3},{3,2},{4,5},{5,4},{6,7},{7,6},{8,9},{9,8},{10,11... | collective-permute-start | bytes 3145736 | tf_op jit(solution)/shard_map/ppermute | solution.py:57
  21.2 0.2 collective-permute-start.3
  21.3 0.0 copy-start.3
  21.3 0.7 copy-done.3
  22.0 0.0 copy-start
  22.0 0.0 copy-start.1
  22.0 0.0 copy-start.6
  22.0 0.0 copy-start.5
  22.0 3.1 %pick.1 = bf16[64,8,128]{2,1,0:T(8,128)(2,1)} custom-call(s32[1]{0:T(128)} %bitcast.1.rank, s32[2,4]{1,0:T(2,128)S(1)} %bitcast.19, bf16[594,5120]{1,0:T(8,128)(2,1)} %refs_7_.1, bf16[594,5120]{1,0:T(8,128)(2,1)} %refs_7_.1, bf16[594,5120]{1,0:T(8,128)(2,1)} %refs_7_.1, bf16[594,5120]{1,0:T(8,128)(2,1)} %refs_7_.1, bf16[594,5120]{1,0:T(8,128)(2,1)} %refs_7_.1, ...), custom_call_target="tpu_custom_call" | custom-call | tf_op jit(solution)/shard_map/pick/pallas_call | solution.py:109
  25.1 0.0 copy-start.2
  25.1 6.6 %all-to-all-start = ((bf16[64,8,128]{2,1,0:T(8,128)(2,1)}), bf16[64,8,128]{2,1,0:T(8,128)(2,1)S(1)}, u32[]{:S(2)}, u32[]{:S(2)}) async-start(bf16[64,8,128]{2,1,0:T(8,128)(2,1)} %pick.1), calls=%async_computation | async-start | bytes 262144 | tf_op jit(solution)/shard_map/all_to_all | solution.py:53
  31.7 0.0 copy-done
  31.7 0.5 collective-permute-start.1
  32.2 0.0 copy-done.1
  32.2 0.2 collective-permute-start.4
  32.4 0.0 copy-done.6
  32.4 0.1 convert_element_type.25
  32.5 0.1 fusion
  32.6 0.1 pad_add_fusion.place
  32.7 0.1 pad_maximum_fusion
  32.8 9.2 %all-to-all-done = bf16[64,8,128]{2,1,0:T(8,128)(2,1)S(1)} async-done(((bf16[64,8,128]{2,1,0:T(8,128)(2,1)}), bf16[64,8,128]{2,1,0:T(8,128)(2,1)S(1)}, u32[]{:S(2)}, u32[]{:S(2)}) %all-to-all-start) | async-done | bytes 131104 | tf_op jit(solution)/shard_map/all_to_all | solution.py:53
  41.9 0.1 convert_reduce_fusion.1.own
  42.0 2.2 %collective-permute-start = (f32[8,128]{1,0:T(8,128)S(1)}, f32[8,128]{1,0:T(8,128)S(1)}, u32[]{:S(2)}, u32[]{:S(2)}) collective-permute-start(f32[8,128]{1,0:T(8,128)S(1)} %convert_reduce_fusion.1.own), channel_id=1, source_target_pairs={{0,1},{1,0},{2,3},{3,2},{4,5},{5,4},{6,7},{7,6},{8,9},{9,8},{10,11... | collective-permute-start | bytes 12296 | tf_op jit(solution)/shard_map/ppermute | solution.py:57
  44.2 0.8 bitcast_convert_fusion.gain
  45.0 0.0 copy-done.5
  45.0 0.1 stack.37.info
  45.1 0.0 collective-permute-done.other
  45.1 0.0 collective-permute-done.1.other_weights
  45.1 0.7 joint.1
  45.8 0.0 collective-permute-done.4.other_weights
  45.8 0.0 collective-permute-done.2.other_keys
  45.9 0.0 copy-start.4
  45.9 0.0 collective-permute-done.3.other_values
  45.9 15.9 %all_to_all.35.got = bf16[64,8,128]{2,1,0:T(8,128)(2,1)S(1)} all-to-all(bf16[64,8,128]{2,1,0:T(8,128)(2,1)S(1)} %get-tuple-element.20), channel_id=1, replica_groups=mesh['parts'=2,'seq_0'=8,'seq_1'=8,'seq_2'=2] {'seq_0','seq_1'}, dimensions={0} | all-to-all | bytes 262144 | tf_op jit(solution)/shard_map/all_to_all | solution.py:53
  61.8 0.0 copy-done.2
  61.8 0.7 rotate.1
  62.5 16.0 %all_to_all.36.heads = bf16[64,8,128]{2,1,0:T(8,128)(2,1)S(1)} all-to-all(bf16[64,8,128]{2,1,0:T(8,128)(2,1)S(1)} %rotate.1), channel_id=1, replica_groups=mesh['parts'=2,'seq_0'=8,'seq_1'=8,'seq_2'=2] {'seq_0','seq_1'}, dimensions={0} | all-to-all | bytes 262144 | tf_op jit(solution)/shard_map/all_to_all | solution.py:53
  78.5 0.0 copy-done.4
  78.5 2.8 %attend.1 = bf16[64,8,128]{2,1,0:T(8,128)(2,1)S(1)} custom-call(s32[6]{0:T(128)S(1)} %stack.37.info, bf16[64,8,128]{2,1,0:T(8,128)(2,1)S(1)} %all_to_all.36.heads, bf16[2,256,1024]{2,1,0:T(8,128)(2,1)} %keys.1, bf16[2,256,1024]{2,1,0:T(8,128)(2,1)} %copy-done.4, bf16[2,256,1024]{2,1,0:T(8,128)(2,1)} %values.1, ...), custom_call_target="tpu_custom_call" | custom-call | tf_op jit(solution)/shard_map/attend/pallas_call | solution.py:455
  81.3 16.1 %all_to_all.37.got = bf16[64,8,128]{2,1,0:T(8,128)(2,1)S(1)} all-to-all(bf16[64,8,128]{2,1,0:T(8,128)(2,1)S(1)} %attend.1), channel_id=1, replica_groups=mesh['parts'=2,'seq_0'=8,'seq_1'=8,'seq_2'=2] {'seq_0','seq_1'}, dimensions={0} | all-to-all | bytes 262144 | tf_op jit(solution)/shard_map/all_to_all | solution.py:53
  97.4 0.4 merge.1
  97.9 15.9 %all_to_all.38.own = bf16[64,8,128]{2,1,0:T(8,128)(2,1)S(1)} all-to-all(bf16[64,8,128]{2,1,0:T(8,128)(2,1)S(1)} %merge.1), channel_id=1, replica_groups=mesh['parts'=2,'seq_0'=8,'seq_1'=8,'seq_2'=2] {'seq_0','seq_1'}, dimensions={0} | all-to-all | bytes 262144 | tf_op jit(solution)/shard_map/all_to_all | solution.py:53
  113.8 5.4 %collective-permute-start.5 = (bf16[64,8,128]{2,1,0:T(8,128)(2,1)S(1)}, bf16[64,8,128]{2,1,0:T(8,128)(2,1)S(1)}, u32[]{:S(2)}, u32[]{:S(2)}) collective-permute-start(bf16[64,8,128]{2,1,0:T(8,128)(2,1)S(1)} %all_to_all.38.own), channel_id=1, source_target_pairs={{0,1},{1,0},{2,3},{3,2},{4,5},{5,4},{6,7},{7,6},{8,9},{9,8},{10,11... | collective-permute-start | bytes 393224 | tf_op jit(solution)/shard_map/ppermute | solution.py:57
  119.2 1.0 collective-permute-done.5.other
  120.2 1.2 project.1
  121.4 15.9 %all_to_all.39.got = bf16[64,8,128]{2,1,0:T(8,128)(2,1)S(1)} all-to-all(bf16[64,8,128]{2,1,0:T(8,128)(2,1)S(1)} %get-tuple-element.30), channel_id=1, replica_groups=mesh['parts'=2,'seq_0'=8,'seq_1'=8,'seq_2'=2] {'seq_0','seq_1'}, dimensions={0} | all-to-all | bytes 262144 | tf_op jit(solution)/shard_map/all_to_all | solution.py:53
  137.2 2.5 %mlp.1 = bf16[64,8,128]{2,1,0:T(8,128)(2,1)S(1)} custom-call(bf16[64,8,128]{2,1,0:T(8,128)(2,1)S(1)} %all_to_all.39.got, f32[1,5120]{1,0:T(1,128)S(1)} %bitcast.17, bf16[5120,128]{1,0:T(8,128)(2,1)} %w_gate.1, bf16[5120,128]{1,0:T(8,128)(2,1)} %w_up.1, bf16[128,5120]{1,0:T(8,128)(2,1)} %w_down.1), custom_call_target="tpu_custom_call" | custom-call | tf_op jit(solution)/shard_map/mlp/pallas_call | solution.py:482
  139.8 16.0 %all_to_all.40 = bf16[64,8,128]{2,1,0:T(8,128)(2,1)S(1)} all-to-all(bf16[64,8,128]{2,1,0:T(8,128)(2,1)S(1)} %mlp.1), channel_id=1, replica_groups=mesh['parts'=2,'seq_0'=8,'seq_1'=8,'seq_2'=2] {'seq_0','seq_1'}, dimensions={0} | all-to-all | bytes 262144 | tf_op jit(solution)/shard_map/all_to_all | solution.py:53
  155.8 0.1 convert_reduce_fusion
  155.9 3.3 %collective-permute-start.6 = (f32[8,128]{1,0:T(8,128)S(1)}, f32[8,128]{1,0:T(8,128)S(1)}, u32[]{:S(2)}, u32[]{:S(2)}) collective-permute-start(f32[8,128]{1,0:T(8,128)S(1)} %convert_reduce_fusion), channel_id=1, source_target_pairs={{0,1},{1,0},{2,3},{3,2},{4,5},{5,4},{6,7},{7,6},{8,9},{9,8},{10,11... | collective-permute-start | bytes 12296 | tf_op jit(solution)/shard_map/ppermute | solution.py:57
  159.1 0.8 collective-permute-done.6
  160.0 0.7 select_convert_fusion
  (5 shorter events, 0.0 us)
Async XLA Ops:
  0.6 45.2 %collective-permute-start.2 = (bf16[2,256,1024]{2,1,0:T(8,128)(2,1)}, bf16[2,256,1024]{2,1,0:T(8,128)(2,1)S(1)}, u32[]{:S(2)}, u32[]{:S(2)}) collective-permute-start(bf16[2,256,1024]{2,1,0:T(8,128)(2,1)} %keys.1), channel_id=1, source_target_pairs={{0,1},{1,0},{2,3},{3,2},{4,5},{5,4},{6,7},{7,6},{8,9},{9,8},{10,11... | collective-permute-start | bytes 3145736 | tf_op jit(solution)/shard_map/ppermute | solution.py:57
  21.2 24.7 %collective-permute-start.3 = (bf16[2,256,1024]{2,1,0:T(8,128)(2,1)}, bf16[2,256,1024]{2,1,0:T(8,128)(2,1)}, u32[]{:S(2)}, u32[]{:S(2)}) collective-permute-start(bf16[2,256,1024]{2,1,0:T(8,128)(2,1)} %values.1), channel_id=1, source_target_pairs={{0,1},{1,0},{2,3},{3,2},{4,5},{5,4},{6,7},{7,6},{8,9},{9,8},{10,11... | collective-permute-start | bytes 3145736 | tf_op jit(solution)/shard_map/ppermute | solution.py:57
  21.3 0.7 copy-start.3
  22.0 9.7 %copy-start = (bf16[40,7168]{1,0:T(8,128)(2,1)S(1)}, bf16[40,7168]{1,0:T(8,128)(2,1)}, u32[]{:S(2)}) copy-start(bf16[40,7168]{1,0:T(8,128)(2,1)} %weights.1) | copy-start | bytes 1720324
  22.0 10.2 %copy-start.1 = (bf16[5120,40]{0,1:T(8,128)(2,1)S(1)}, bf16[5120,40]{0,1:T(8,128)(2,1)}, u32[]{:S(2)}) copy-start(bf16[5120,40]{0,1:T(8,128)(2,1)} %param.21) | copy-start | bytes 1228804
  22.0 10.4 %copy-start.6 = (s32[2]{0:T(128)S(1)}, s32[2]{0:T(128)}, u32[]{:S(2)}) copy-start(s32[2]{0:T(128)} %param.14) | copy-start | bytes 28
  22.0 23.0 %copy-start.5 = (bf16[5120]{0:T(1024)(128)(2,1)S(1)}, bf16[5120]{0:T(1024)(128)(2,1)}, u32[]{:S(2)}) copy-start(bf16[5120]{0:T(1024)(128)(2,1)} %param.22) | copy-start | bytes 30724
  25.1 36.7 %copy-start.2 = (f32[7168]{0:T(1024)S(1)}, f32[7168]{0:T(1024)}, u32[]{:S(2)}) copy-start(f32[7168]{0:T(1024)} %param.18) | copy-start | bytes 86020
  25.1 16.8 %all-to-all-start = ((bf16[64,8,128]{2,1,0:T(8,128)(2,1)}), bf16[64,8,128]{2,1,0:T(8,128)(2,1)S(1)}, u32[]{:S(2)}, u32[]{:S(2)}) async-start(bf16[64,8,128]{2,1,0:T(8,128)(2,1)} %pick.1), calls=%async_computation | async-start | bytes 262144 | tf_op jit(solution)/shard_map/all_to_all | solution.py:53
  31.7 13.4 %collective-permute-start.1 = (bf16[40,7168]{1,0:T(8,128)(2,1)S(1)}, bf16[40,7168]{1,0:T(8,128)(2,1)S(1)}, u32[]{:S(2)}, u32[]{:S(2)}) collective-permute-start(bf16[40,7168]{1,0:T(8,128)(2,1)S(1)} %copy-done), channel_id=1, source_target_pairs={{0,1},{1,0},{2,3},{3,2},{4,5},{5,4},{6,7},{7,6},{8,9},{9,8},{10,11... | collective-permute-start | bytes 1720328 | tf_op jit(solution)/shard_map/ppermute | solution.py:57
  32.2 13.6 %collective-permute-start.4 = (bf16[40,5120]{1,0:T(8,128)(2,1)S(1)}, bf16[40,5120]{1,0:T(8,128)(2,1)S(1)}, u32[]{:S(2)}, u32[]{:S(2)}) collective-permute-start(bf16[40,5120]{1,0:T(8,128)(2,1)S(1)} %bitcast.15), channel_id=1, source_target_pairs={{0,1},{1,0},{2,3},{3,2},{4,5},{5,4},{6,7},{7,6},{8,9},{9,8},{10,11... | collective-permute-start | bytes 1228808 | tf_op jit(solution)/shard_map/ppermute | solution.py:57
  42.0 3.1 %collective-permute-start = (f32[8,128]{1,0:T(8,128)S(1)}, f32[8,128]{1,0:T(8,128)S(1)}, u32[]{:S(2)}, u32[]{:S(2)}) collective-permute-start(f32[8,128]{1,0:T(8,128)S(1)} %convert_reduce_fusion.1.own), channel_id=1, source_target_pairs={{0,1},{1,0},{2,3},{3,2},{4,5},{5,4},{6,7},{7,6},{8,9},{9,8},{10,11... | collective-permute-start | bytes 12296 | tf_op jit(solution)/shard_map/ppermute | solution.py:57
  45.9 32.6 %copy-start.4 = (bf16[2,256,1024]{2,1,0:T(8,128)(2,1)}, bf16[2,256,1024]{2,1,0:T(8,128)(2,1)S(1)}, u32[]{:S(2)}) copy-start(bf16[2,256,1024]{2,1,0:T(8,128)(2,1)S(1)} %collective-permute-done.2.other_keys) | copy-start | bytes 3145732
  113.8 6.4 %collective-permute-start.5 = (bf16[64,8,128]{2,1,0:T(8,128)(2,1)S(1)}, bf16[64,8,128]{2,1,0:T(8,128)(2,1)S(1)}, u32[]{:S(2)}, u32[]{:S(2)}) collective-permute-start(bf16[64,8,128]{2,1,0:T(8,128)(2,1)S(1)} %all_to_all.38.own), channel_id=1, source_target_pairs={{0,1},{1,0},{2,3},{3,2},{4,5},{5,4},{6,7},{7,6},{8,9},{9,8},{10,11... | collective-permute-start | bytes 393224 | tf_op jit(solution)/shard_map/ppermute | solution.py:57
  155.9 4.1 %collective-permute-start.6 = (f32[8,128]{1,0:T(8,128)S(1)}, f32[8,128]{1,0:T(8,128)S(1)}, u32[]{:S(2)}, u32[]{:S(2)}) collective-permute-start(f32[8,128]{1,0:T(8,128)S(1)} %convert_reduce_fusion), channel_id=1, source_target_pairs={{0,1},{1,0},{2,3},{3,2},{4,5},{5,4},{6,7},{7,6},{8,9},{9,8},{10,11... | collective-permute-start | bytes 12296 | tf_op jit(solution)/shard_map/ppermute | solution.py:57
